TPU v7x, 32 devices: a whole 2x2x4 slice. The times are simulated.
32 devices in a mesh: seq: 8 (over z, y), shard: 4 (over x, core).
Axes of the slice: x: 2, y: 2, z: 4, core: 2. Of those that a mesh axis runs over, the one named last changes fastest.
Arguments:
- tokens: bfloat16 [8, 4096, 768], P('shard', 'seq'), may hold values from -6 to 6
- segments: int32 [8, 4096], P('shard'), may hold values from 0 to 20, as said below
- positions: int32 [8, 4096], P('shard', 'seq'), may hold values from 0 to 1999, as said below
- cotangent: bfloat16 [8, 4096, 768], P('shard', 'seq'), may hold values from -6 to 6
- w_qkv: bfloat16 [768, 2304], P('shard'), may hold values from -0.21875 to 0.21875
- w_out: bfloat16 [768, 768], P('shard'), may hold values from -3 to 3
- w_gate: bfloat16 [768, 3072], P('shard'), may hold values from -0.21875 to 0.21875
- w_up: bfloat16 [768, 3072], P('shard'), may hold values from -0.21875 to 0.21875
- w_down: bfloat16 [3072, 768], P('shard'), may hold values from -0.109375 to 0.109375
- ln1_gain: bfloat16 [768], P('shard'), may hold values from 0.099609375 to 1.8984375
- ln1_bias: bfloat16 [768], P('shard'), may hold values from -3 to 3
- ln2_gain: bfloat16 [768], P('shard'), may hold values from 0.099609375 to 1.8984375
- ln2_bias: bfloat16 [768], P('shard'), may hold values from -3 to 3
Outputs:
- output: bfloat16 [8, 4096, 768], P('shard', 'seq')
- input_grad: bfloat16 [8, 4096, 768], P('shard', 'seq')
- grad_w_qkv: float32 [768, 2304], P('shard')
- grad_w_out: float32 [768, 768], P('shard')
- grad_w_gate: float32 [768, 3072], P('shard')
- grad_w_up: float32 [768, 3072], P('shard')
- grad_w_down: float32 [3072, 768], P('shard')
- grad_ln1_gain: float32 [768], P('shard')
- grad_ln1_bias: float32 [768], P('shard')
- grad_ln2_gain: float32 [768], P('shard')
- grad_ln2_bias: float32 [768], P('shard')
Inputs may be any that keep to these rules, and one draw needn't show every extreme that they name: segments[s, t] numbers the documents of sequence s in order from 0 and never falls along t; every document has 200 to 2000 tokens, except that the end of the sequence may cut the last one short. positions[s, t] counts the earlier tokens of the same document of sequence s.
All inputs are finite; a program needn't handle non-finite values.
Results may differ from a plain program's by a relative error of at most 0.025.
Values may be sent and summed in bfloat16 or wider, within the bound.
A program may use at most 256 MiB of HBM per device.

v0:
```python
import functools
import math

import jax
import jax.numpy as jnp
from jax import lax
from jax.experimental import pallas as pl
from jax.experimental.pallas import tpu as pltpu
from jax.sharding import PartitionSpec as P

HEADS = 12
HD = 64


EPS = 1e-05
ROPE_BASE = 1000.0


def rope_tables(pos_block):
    half_dim = HD // 2
    freqs = jnp.exp(jnp.arange(half_dim, dtype=jnp.float32) * (-math.log(ROPE_BASE) / half_dim))
    angle = pos_block.astype(jnp.float32)[..., None] * freqs
    return (jnp.cos(angle)[:, :, None, :], jnp.sin(angle)[:, :, None, :])


def rotate(heads, cos_b, sin_b):
    half_dim = heads.shape[-1] // 2
    first = heads[..., :half_dim]
    second = heads[..., half_dim:]
    return jnp.concatenate(
        [first * cos_b - second * sin_b, second * cos_b + first * sin_b], axis=-1
    )


def rotate_back(grads, cos_b, sin_b):
    half_dim = grads.shape[-1] // 2
    first = grads[..., :half_dim]
    second = grads[..., half_dim:]
    return jnp.concatenate(
        [first * cos_b + second * sin_b, second * cos_b - first * sin_b], axis=-1
    )


def norm_fwd(values, gain, bias):
    mean_val = jnp.mean(values, axis=-1, keepdims=True)
    centered = values - mean_val
    variance = jnp.mean(centered * centered, axis=-1, keepdims=True)
    inverse = lax.rsqrt(variance + EPS)
    normed = centered * inverse
    return (normed * gain + bias, normed, inverse)


def norm_back(grad_in, normed, inverse, gain):
    scaled = grad_in * gain
    return inverse * (
        scaled
        - jnp.mean(scaled, axis=-1, keepdims=True)
        - normed * jnp.mean(scaled * normed, axis=-1, keepdims=True)
    )


def head_split(block_rows, seq_count, row_count):
    return block_rows.reshape(seq_count, row_count, HEADS, HD)


def attend(q_heads, q_seg, k_full, v_full, seg_all, block, score_scale):
    seq_count, row_count = (q_heads.shape[0], q_heads.shape[1])
    block_count = k_full.shape[1] // block

    def attend_step(carry, index):
        row_total, value_sum = carry
        start = index * block
        k_part = head_split(lax.dynamic_slice_in_dim(k_full, start, block, 1), seq_count, block)
        v_part = head_split(lax.dynamic_slice_in_dim(v_full, start, block, 1), seq_count, block)
        seg_part = lax.dynamic_slice_in_dim(seg_all, start, block, 1)
        raw = (
            jnp.einsum("sqhd,skhd->shqk", q_heads, k_part, preferred_element_type=jnp.float32)
            * score_scale
        )
        same_doc = q_seg[:, None, :, None] == seg_part[:, None, None, :]
        expo = jnp.where(same_doc, jnp.exp(raw), 0.0)
        row_total = row_total + jnp.sum(expo, axis=-1)
        value_sum = value_sum + jnp.einsum(
            "shqk,skhd->sqhd", expo.astype(jnp.bfloat16), v_part, preferred_element_type=jnp.float32
        )
        return ((row_total, value_sum), None)

    start_carry = (
        jnp.zeros((seq_count, HEADS, row_count), jnp.float32),
        jnp.zeros((seq_count, row_count, HEADS, HD), jnp.float32),
    )
    final, unused = lax.scan(attend_step, start_carry, jnp.arange(block_count, dtype=jnp.int32))
    return final


def back_keys(q_heads, g_heads, delta, q_seg, k_full, v_full, seg_all, block, score_scale):
    seq_count, row_count = (q_heads.shape[0], q_heads.shape[1])
    full_len = k_full.shape[1]
    block_count = full_len // block

    def back_step(carry, index):
        start = index * block
        k_part = head_split(lax.dynamic_slice_in_dim(k_full, start, block, 1), seq_count, block)
        v_part = head_split(lax.dynamic_slice_in_dim(v_full, start, block, 1), seq_count, block)
        seg_part = lax.dynamic_slice_in_dim(seg_all, start, block, 1)
        raw = (
            jnp.einsum("sqhd,skhd->shqk", q_heads, k_part, preferred_element_type=jnp.float32)
            * score_scale
        )
        same_doc = q_seg[:, None, :, None] == seg_part[:, None, None, :]
        expo = jnp.where(same_doc, jnp.exp(raw), 0.0)
        prob_grad = jnp.einsum(
            "sqhd,skhd->shqk", g_heads, v_part, preferred_element_type=jnp.float32
        )
        d_score = (expo * (prob_grad - delta[..., None])).astype(jnp.bfloat16)
        q_grad = carry[0] + jnp.einsum(
            "shqk,skhd->sqhd", d_score, k_part, preferred_element_type=jnp.float32
        )
        k_grad = (
            jnp.einsum("shqk,sqhd->skhd", d_score, q_heads, preferred_element_type=jnp.float32)
            * score_scale
        )
        v_grad = jnp.einsum(
            "shqk,sqhd->skhd",
            expo.astype(jnp.bfloat16),
            g_heads,
            preferred_element_type=jnp.float32,
        )
        k_store = lax.dynamic_update_slice_in_dim(
            carry[1], k_grad.reshape(seq_count, block, HEADS * HD), start, 1
        )
        v_store = lax.dynamic_update_slice_in_dim(
            carry[2], v_grad.reshape(seq_count, block, HEADS * HD), start, 1
        )
        return ((q_grad, k_store, v_store), None)

    q_zero = jnp.zeros((seq_count, row_count, HEADS, HD), jnp.float32)
    kv_zero = jnp.zeros((seq_count, full_len, HEADS * HD), jnp.float32)
    start_carry = (q_zero, kv_zero, kv_zero)
    final, unused = lax.scan(back_step, start_carry, jnp.arange(block_count, dtype=jnp.int32))
    return (final[0] * score_scale,) + tuple(final[1:])


def local(
    tokens,
    segments,
    positions,
    cotangent,
    w_qkv,
    w_out,
    w_gate,
    w_up,
    w_down,
    ln1_gain,
    ln1_bias,
    ln2_gain,
    ln2_bias,
):
    seq_count, row_count, model_width = tokens.shape
    score_scale = HD ** (-0.5)
    q_seg = lax.dynamic_slice_in_dim(segments, lax.axis_index("seq") * row_count, row_count, 1)
    gathered = (
        lax.all_gather(w_qkv, "shard", axis=0, tiled=True),
        lax.all_gather(w_out, "shard", axis=0, tiled=True),
        lax.all_gather(w_gate, "shard", axis=0, tiled=True),
        lax.all_gather(w_up, "shard", axis=0, tiled=True),
        lax.all_gather(w_down, "shard", axis=0, tiled=True),
        lax.all_gather(ln1_gain, "shard", axis=0, tiled=True),
        lax.all_gather(ln1_bias, "shard", axis=0, tiled=True),
        lax.all_gather(ln2_gain, "shard", axis=0, tiled=True),
        lax.all_gather(ln2_bias, "shard", axis=0, tiled=True),
    )
    full_qkv, full_out, full_gate, full_up, full_down, gain_one, bias_one, gain_two, bias_two = (
        gathered
    )
    cos_b, sin_b = rope_tables(positions)
    qkv_all = jnp.einsum("scd,de->sce", tokens, full_qkv, preferred_element_type=jnp.float32)
    q_heads = rotate(
        head_split(qkv_all[..., :model_width], seq_count, row_count), cos_b, sin_b
    ).astype(jnp.bfloat16)
    k_heads = rotate(
        head_split(qkv_all[..., model_width : 2 * model_width], seq_count, row_count), cos_b, sin_b
    ).astype(jnp.bfloat16)
    v_heads = head_split(qkv_all[..., 2 * model_width :], seq_count, row_count).astype(jnp.bfloat16)
    k_local = k_heads.reshape(seq_count, row_count, model_width)
    v_local = v_heads.reshape(seq_count, row_count, model_width)
    k_full, v_full = (
        lax.all_gather(k_local, "seq", axis=1, tiled=True),
        lax.all_gather(v_local, "seq", axis=1, tiled=True),
    )
    row_total, value_sum = attend(q_heads, q_seg, k_full, v_full, segments, row_count, score_scale)
    denom = jnp.transpose(row_total, (0, 2, 1))[..., None]
    attn_out = value_sum / denom
    joined = attn_out.reshape(seq_count, row_count, model_width).astype(jnp.bfloat16)
    tokens_f = tokens.astype(jnp.float32)
    h_one = tokens_f + jnp.einsum(
        "sci,io->sco", joined, full_out, preferred_element_type=jnp.float32
    )
    x_one, normed_one, inverse_one = norm_fwd(
        h_one, gain_one.astype(jnp.float32), bias_one.astype(jnp.float32)
    )
    x_low = x_one.astype(jnp.bfloat16)
    gate_pre = jnp.einsum("scd,df->scf", x_low, full_gate, preferred_element_type=jnp.float32)
    up_pre = jnp.einsum("scd,df->scf", x_low, full_up, preferred_element_type=jnp.float32)
    sigma = jax.nn.sigmoid(gate_pre)
    smooth = gate_pre * sigma
    hidden = (smooth * up_pre).astype(jnp.bfloat16)
    h_two = x_one + jnp.einsum("scf,fd->scd", hidden, full_down, preferred_element_type=jnp.float32)
    result, normed_two, inverse_two = norm_fwd(
        h_two, gain_two.astype(jnp.float32), bias_two.astype(jnp.float32)
    )
    output = result.astype(jnp.bfloat16)
    regathered = (
        lax.all_gather(w_qkv, "shard", axis=0, tiled=True),
        lax.all_gather(w_out, "shard", axis=0, tiled=True),
        lax.all_gather(w_gate, "shard", axis=0, tiled=True),
        lax.all_gather(w_up, "shard", axis=0, tiled=True),
        lax.all_gather(w_down, "shard", axis=0, tiled=True),
        lax.all_gather(ln1_gain, "shard", axis=0, tiled=True),
        lax.all_gather(ln2_gain, "shard", axis=0, tiled=True),
    )
    back_qkv, back_out, back_gate, back_up, back_down, back_gain_one, back_gain_two = regathered
    back_k, back_v = (
        lax.all_gather(k_local, "seq", axis=1, tiled=True),
        lax.all_gather(v_local, "seq", axis=1, tiled=True),
    )
    cot_f = cotangent.astype(jnp.float32)
    grad_gain_two = jnp.sum(cot_f * normed_two, axis=(0, 1))
    grad_bias_two = jnp.sum(cot_f, axis=(0, 1))
    dh_two = norm_back(cot_f, normed_two, inverse_two, back_gain_two.astype(jnp.float32))
    dm_low = dh_two.astype(jnp.bfloat16)
    grad_down = jnp.einsum("scf,scd->fd", hidden, dm_low, preferred_element_type=jnp.float32)
    d_hidden = jnp.einsum("scd,fd->scf", dm_low, back_down, preferred_element_type=jnp.float32)
    d_up = (d_hidden * smooth).astype(jnp.bfloat16)
    d_gate = (d_hidden * up_pre * sigma * (1.0 + gate_pre * (1.0 - sigma))).astype(jnp.bfloat16)
    grad_gate = jnp.einsum("scd,scf->df", x_low, d_gate, preferred_element_type=jnp.float32)
    grad_up = jnp.einsum("scd,scf->df", x_low, d_up, preferred_element_type=jnp.float32)
    dx_one = (
        dh_two
        + jnp.einsum("scf,df->scd", d_gate, back_gate, preferred_element_type=jnp.float32)
        + jnp.einsum("scf,df->scd", d_up, back_up, preferred_element_type=jnp.float32)
    )
    grad_gain_one = jnp.sum(dx_one * normed_one, axis=(0, 1))
    grad_bias_one = jnp.sum(dx_one, axis=(0, 1))
    dh_one = norm_back(dx_one, normed_one, inverse_one, back_gain_one.astype(jnp.float32))
    d_attn = dh_one.astype(jnp.bfloat16)
    grad_out = jnp.einsum("sci,sco->io", joined, d_attn, preferred_element_type=jnp.float32)
    d_joined = jnp.einsum(
        "sco,io->sci", d_attn, back_out, preferred_element_type=jnp.float32
    ).astype(jnp.bfloat16)
    d_heads = head_split(d_joined, seq_count, row_count).astype(jnp.float32)
    g_heads = (d_heads / denom).astype(jnp.bfloat16)
    delta = jnp.transpose(jnp.sum(d_heads * attn_out, axis=-1) / denom[..., 0], (0, 2, 1))
    q_grad, k_all, v_all = back_keys(
        q_heads, g_heads, delta, q_seg, back_k, back_v, segments, row_count, score_scale
    )
    k_sum, v_sum = (
        lax.psum_scatter(k_all.astype(jnp.bfloat16), "seq", scatter_dimension=1, tiled=True).astype(
            jnp.float32
        ),
        lax.psum_scatter(v_all.astype(jnp.bfloat16), "seq", scatter_dimension=1, tiled=True).astype(
            jnp.float32
        ),
    )
    k_grad = head_split(k_sum, seq_count, row_count)
    v_grad = head_split(v_sum, seq_count, row_count)
    q_back = rotate_back(q_grad, cos_b, sin_b).reshape(seq_count, row_count, model_width)
    k_back = rotate_back(k_grad, cos_b, sin_b).reshape(seq_count, row_count, model_width)
    d_qkv = jnp.concatenate(
        [q_back, k_back, v_grad.reshape(seq_count, row_count, model_width)], axis=-1
    ).astype(jnp.bfloat16)
    grad_qkv = jnp.einsum("scd,sce->de", tokens, d_qkv, preferred_element_type=jnp.float32)
    d_tokens = dh_one + jnp.einsum(
        "sce,de->scd", d_qkv, back_qkv, preferred_element_type=jnp.float32
    )
    input_grad = d_tokens.astype(jnp.bfloat16)
    owned = (
        lax.psum_scatter(
            grad_qkv.astype(jnp.bfloat16), "shard", scatter_dimension=0, tiled=True
        ).astype(jnp.float32),
        lax.psum_scatter(
            grad_out.astype(jnp.bfloat16), "shard", scatter_dimension=0, tiled=True
        ).astype(jnp.float32),
        lax.psum_scatter(
            grad_gate.astype(jnp.bfloat16), "shard", scatter_dimension=0, tiled=True
        ).astype(jnp.float32),
        lax.psum_scatter(
            grad_up.astype(jnp.bfloat16), "shard", scatter_dimension=0, tiled=True
        ).astype(jnp.float32),
        lax.psum_scatter(
            grad_down.astype(jnp.bfloat16), "shard", scatter_dimension=0, tiled=True
        ).astype(jnp.float32),
        lax.psum_scatter(
            grad_gain_one.astype(jnp.bfloat16), "shard", scatter_dimension=0, tiled=True
        ).astype(jnp.float32),
        lax.psum_scatter(
            grad_bias_one.astype(jnp.bfloat16), "shard", scatter_dimension=0, tiled=True
        ).astype(jnp.float32),
        lax.psum_scatter(
            grad_gain_two.astype(jnp.bfloat16), "shard", scatter_dimension=0, tiled=True
        ).astype(jnp.float32),
        lax.psum_scatter(
            grad_bias_two.astype(jnp.bfloat16), "shard", scatter_dimension=0, tiled=True
        ).astype(jnp.float32),
    )
    summed = (
        lax.psum(owned[0].astype(jnp.bfloat16), "seq").astype(jnp.float32),
        lax.psum(owned[1].astype(jnp.bfloat16), "seq").astype(jnp.float32),
        lax.psum(owned[2].astype(jnp.bfloat16), "seq").astype(jnp.float32),
        lax.psum(owned[3].astype(jnp.bfloat16), "seq").astype(jnp.float32),
        lax.psum(owned[4].astype(jnp.bfloat16), "seq").astype(jnp.float32),
        lax.psum(owned[5].astype(jnp.bfloat16), "seq").astype(jnp.float32),
        lax.psum(owned[6].astype(jnp.bfloat16), "seq").astype(jnp.float32),
        lax.psum(owned[7].astype(jnp.bfloat16), "seq").astype(jnp.float32),
        lax.psum(owned[8].astype(jnp.bfloat16), "seq").astype(jnp.float32),
    )
    return (
        output,
        input_grad,
        summed[0],
        summed[1],
        summed[2],
        summed[3],
        summed[4],
        summed[5],
        summed[6],
        summed[7],
        summed[8],
    )


SEQS_HELD = 2
SEQ_SIZE = 8
GROUPS = 4
LANES = 128
LOG2E = 1.4426950408889634
LN2 = 0.6931471805599453
FAR = 2.0**30
F32 = jnp.float32
BF16 = jnp.bfloat16
VMEM_LIMIT = 60 * 1024 * 1024
FEED_LIMIT = 63 * 1024 * 1024
BY_MESH = pl.DeviceIdType.MESH
BY_LANES = (((1,), (1,)), ((), ()))


def packed_heads(rows):
    return rows + rows // 2


def unpack_heads(block):
    rows = block.shape[0] * 2 // 3
    last = block[rows:]
    third = jnp.concatenate([last[:, :HD], last[:, HD:]], axis=0)
    return jnp.concatenate([block[:rows], third], axis=1)


def pack_heads(value):
    rows = value.shape[0]
    third = value[:, 2 * HD :]
    return value[:, : 2 * HD], jnp.concatenate([third[: rows // 2], third[rows // 2 :]], axis=1)


def flip(index, bit):
    return index + bit - 2 * bit * lax.rem(lax.div(index, bit), 2)


def gather_kernel(
    chunks, by_z, tok_ref, w_ref, n_ref, place_ref, freq_ref, all_ref, w_all_ref, n_all_ref, turn_ref, send, recv, kept, w_send, w_recv
):
    me = lax.axis_index("seq")
    shard = lax.axis_index("shard")
    shards = w_all_ref.shape[0]
    half = lax.div(me, GROUPS)
    y_near, z_near, partner = flip(me, 1), flip(me, 2), flip(me, 4)
    barrier = pltpu.get_barrier_semaphore()
    for device in (y_near, z_near, partner):
        pl.semaphore_signal(barrier, inc=1, device_id={"seq": device}, device_id_type=BY_MESH)
    for step in range(1, shards):
        pl.semaphore_signal(
            barrier, inc=1, device_id={"shard": lax.rem(shard + step, shards)}, device_id_type=BY_MESH
        )
    pl.semaphore_wait(barrier, 2 + shards)

    part = tok_ref.shape[1] // chunks
    started = []

    def go(source, target, slot, device):
        copy = pltpu.make_async_remote_copy(
            src_ref=source,
            dst_ref=target,
            send_sem=send.at[slot],
            recv_sem=recv.at[slot],
            device_id={"seq": device},
            device_id_type=BY_MESH,
        )
        copy.start()
        started.append(copy)
        return copy

    def rows(chunk):
        return pl.ds(chunk * part, part)

    def relay(piece, chunk, slot, device):
        return go(all_ref.at[piece, rows(chunk)], all_ref.at[piece, rows(chunk)], slot * chunks + chunk, device)

    def own(which, chunk, slot, device):
        return go(tok_ref.at[which, rows(chunk)], all_ref.at[me, rows(chunk)], slot * chunks + chunk, device)

    crossing = [own(1 - half, chunk, 0, partner) for chunk in range(chunks)]
    own_y, own_z = [], []
    for chunk in range(chunks):
        own_y.append(own(half, chunk, 1, y_near))
        own_z.append(own(half, chunk, 2, z_near))
    weights = []
    for step in range(1, shards):
        copy = pltpu.make_async_remote_copy(
            src_ref=w_ref,
            dst_ref=w_all_ref.at[shard],
            send_sem=w_send.at[step],
            recv_sem=w_recv.at[step],
            device_id={"shard": lax.rem(shard + step, shards)},
            device_id_type=BY_MESH,
        )
        copy.start()
        weights.append(copy)
        copy = pltpu.make_async_remote_copy(
            src_ref=n_ref,
            dst_ref=n_all_ref.at[shard],
            send_sem=w_send.at[shards + step],
            recv_sem=w_recv.at[shards + step],
            device_id={"shard": lax.rem(shard + step, shards)},
            device_id_type=BY_MESH,
        )
        copy.start()
        weights.append(copy)
    keep_n = pltpu.make_async_copy(n_ref, n_all_ref.at[shard], kept.at[2])
    keep_n.start()
    keep_tok = pltpu.make_async_copy(tok_ref.at[half], all_ref.at[me], kept.at[0])
    keep_tok.start()
    keep_w = pltpu.make_async_copy(w_ref, w_all_ref.at[shard], kept.at[1])
    keep_w.start()

    def turn_piece(index, carry):
        count = turn_ref.shape[0] // place_ref.shape[0]
        lane = lax.broadcasted_iota(jnp.int32, (count, LANES), 1)
        place = jnp.transpose(jnp.broadcast_to(place_ref[index], (LANES, count)))
        angle = place * freq_ref[...]
        turn_ref[pl.ds(pl.multiple_of(index * count, count), count), :] = jnp.where(
            lane < HD, jnp.cos(angle), jnp.sin(angle)
        )
        return carry

    lax.fori_loop(0, place_ref.shape[0], turn_piece, 0)

    cross_y, cross_z, corner = [], [], []
    for chunk in range(chunks):
        own_y[chunk].wait_recv()
        if chunk < by_z:
            corner.append(relay(y_near, chunk, 5, z_near))
        own_z[chunk].wait_recv()
        if chunk >= by_z:
            corner.append(relay(z_near, chunk, 5, y_near))
        crossing[chunk].wait_recv()
        cross_y.append(relay(partner, chunk, 3, y_near))
        cross_z.append(relay(partner, chunk, 4, z_near))
    for chunk in range(chunks):
        cross_y[chunk].wait_recv()
        if chunk < by_z:
            corner.append(relay(flip(y_near, 4), chunk, 6, z_near))
        cross_z[chunk].wait_recv()
        if chunk >= by_z:
            corner.append(relay(flip(z_near, 4), chunk, 6, y_near))
    for copy in corner:
        copy.wait_recv()
    for copy in weights:
        copy.wait()
    keep_tok.wait()
    keep_w.wait()
    keep_n.wait()
    for copy in started:
        copy.wait_send()


def gather_tokens(tokens, w_part, norms, place, freq, shards, chunks=8, by_z=3):
    seqs, rows, width = tokens.shape
    anywhere = pl.BlockSpec(memory_space=pl.ANY)
    vmem = pl.BlockSpec(memory_space=pltpu.VMEM)
    return pl.pallas_call(
        functools.partial(gather_kernel, chunks, by_z),
        out_shape=(
            jax.ShapeDtypeStruct((SEQ_SIZE, rows, width), tokens.dtype),
            jax.ShapeDtypeStruct((shards,) + w_part.shape, w_part.dtype),
            jax.ShapeDtypeStruct((shards,) + norms.shape, norms.dtype),
            jax.ShapeDtypeStruct((place.shape[0] * place.shape[2], LANES), F32),
        ),
        in_specs=[anywhere, anywhere, anywhere, vmem, vmem],
        out_specs=(anywhere, anywhere, anywhere, vmem),
        scratch_shapes=[
            pltpu.SemaphoreType.DMA((7 * chunks,)),
            pltpu.SemaphoreType.DMA((7 * chunks,)),
            pltpu.SemaphoreType.DMA((3,)),
            pltpu.SemaphoreType.DMA((2 * shards,)),
            pltpu.SemaphoreType.DMA((2 * shards,)),
        ],
        compiler_params=pltpu.CompilerParams(collective_id=1, has_side_effects=True),
        name="gather_tokens",
    )(tokens, w_part, norms, place, freq)


def project_kernel(seg_ref, turn_ref, x_ref, w_ref, q_ref, k_ref, v_ref):
    rows = x_ref.shape[1]
    held = q_ref.shape[0]
    lane = lax.broadcasted_iota(jnp.int32, (rows, LANES), 1)
    seg = jnp.transpose(jnp.broadcast_to(seg_ref[0], (LANES, rows)))
    turn = turn_ref[...]
    cos_b = jnp.where(lane < HD, turn, 0.0)
    sin_b = jnp.where(lane < HD, pltpu.roll(turn, HD, 1), 0.0)
    sin_b = jnp.where(lane < HD // 2, -sin_b, sin_b)
    same = seg == (lane - HD).astype(F32)
    q_tail = jnp.where(same, 1.0, 0.0)
    k_tail = jnp.where(same | (lane < HD), 0.0, -FAR)
    v_tail = jnp.where(lane < HD, 0.0, 1.0)
    scale = HD ** (-0.5) * LOG2E
    q_cos, q_sin = cos_b * scale, sin_b * scale
    width = held * LANES
    for part in range(3):
        mixed = jnp.dot(x_ref[0], w_ref[:, part * width : (part + 1) * width], preferred_element_type=F32)
        for head in range(held):
            value = mixed[:, head * LANES : (head + 1) * LANES]
            if part == 0:
                value = value * q_cos + pltpu.roll(value, HD // 2, 1) * q_sin + q_tail
                q_ref[head] = value.astype(BF16)
            elif part == 1:
                value = value * cos_b + pltpu.roll(value, HD // 2, 1) * sin_b + k_tail
                k_ref[head] = value.astype(BF16)
            else:
                v_ref[head] = (value + v_tail).astype(BF16)


def project_heads(seg_row, turn, pieces, w_full, held):
    count, rows, width = pieces.shape
    length = count * rows
    row_spec = pl.BlockSpec((1, 1, rows), lambda i: (i, 0, 0))
    head_spec = pl.BlockSpec((held, rows, LANES), lambda i: (0, i, 0))
    head_shape = jax.ShapeDtypeStruct((held, length, LANES), BF16)
    return pl.pallas_call(
        project_kernel,
        out_shape=(head_shape, head_shape, head_shape),
        grid=(count,),
        in_specs=[
            row_spec,
            pl.BlockSpec((rows, LANES), lambda i: (i, 0)),
            pl.BlockSpec((1, rows, width), lambda i: (i, 0, 0)),
            pl.BlockSpec(w_full.shape, lambda i: (0, 0)),
        ],
        out_specs=(head_spec, head_spec, head_spec),
        compiler_params=pltpu.CompilerParams(vmem_limit_bytes=VMEM_LIMIT),
        cost_estimate=pl.CostEstimate(
            flops=2 * length * width * w_full.shape[1],
            bytes_accessed=length * (width * 2 + held * LANES * 6 + LANES * 4),
            transcendentals=length * LANES,
        ),
        name="project_heads",
    )(seg_row.reshape(count, 1, rows), turn, pieces, w_full)


def document_bounds(seg_row, rows):
    first = seg_row[::rows]
    last = seg_row[rows - 1 :: rows]
    low = jnp.sum((seg_row[None, :] < first[:, None]).astype(jnp.int32), axis=1)
    high = jnp.sum((seg_row[None, :] <= last[:, None]).astype(jnp.int32), axis=1)
    return low, high


def windows(bounds, length, window, align):
    low = bounds[0] // align * align
    count = (bounds[1] - low + window - 1) // window
    return jnp.minimum(low, length - count * window), count


def attend_kernel(window, align, low_ref, count_ref, q_ref, k_ref, v_ref, sum_ref, joined_ref):
    block = pl.program_id(0)
    low = low_ref[block]
    sum_ref[...] = jnp.zeros_like(sum_ref)

    def step(index, carry):
        start = pl.multiple_of(low + index * window, align)
        for head in range(q_ref.shape[0]):
            k_part = k_ref[head, pl.ds(start, window), :]
            v_part = v_ref[head, pl.ds(start, window), :]
            score = lax.dot_general(q_ref[head], k_part, BY_LANES, preferred_element_type=F32)
            expo = jnp.exp2(score).astype(BF16)
            sum_ref[head] += jnp.dot(expo, v_part, preferred_element_type=F32)
        return carry

    lax.fori_loop(0, count_ref[block], step, 0)
    rows = q_ref.shape[1]
    parts = [sum_ref[head][:, :HD] / sum_ref[head][:, HD : HD + 1] for head in range(q_ref.shape[0])]
    first, last = pack_heads(jnp.concatenate(parts, axis=1))
    joined_ref[0, :rows] = first.astype(BF16)
    joined_ref[0, rows:] = last.astype(BF16)


def attend_heads(bounds, q_ext, k_ext, v_ext, rows, window=1024, align=16):
    heads, length, lanes = q_ext.shape
    low, count = windows(bounds, length, window, align)
    whole = pl.BlockSpec((heads, length, lanes), lambda i, *_: (0, 0, 0))
    part = pl.BlockSpec((heads, rows, lanes), lambda i, *_: (0, i, 0))
    return pl.pallas_call(
        functools.partial(attend_kernel, window, align),
        out_shape=(
            jax.ShapeDtypeStruct((heads, length, lanes), F32),
            jax.ShapeDtypeStruct((length // rows, packed_heads(rows), LANES), BF16),
        ),
        grid_spec=pltpu.PrefetchScalarGridSpec(
            num_scalar_prefetch=2,
            grid=(length // rows,),
            in_specs=[part, whole, whole],
            out_specs=(part, pl.BlockSpec((1, packed_heads(rows), LANES), lambda i, *_: (i, 0, 0))),
        ),
        compiler_params=pltpu.CompilerParams(vmem_limit_bytes=VMEM_LIMIT),
        cost_estimate=pl.CostEstimate(
            flops=heads * length * length * 4 * lanes // 2,
            bytes_accessed=heads * length * lanes * 10,
            transcendentals=heads * length * length // 2,
        ),
        name="attend_heads",
    )(low, count, q_ext, k_ext, v_ext)


def attend_back_kernel(
    align,
    low_ref,
    count_ref,
    q_ref,
    sum_ref,
    dout_ref,
    turn_ref,
    k_ref,
    v_ref,
    d_ref,
    dq_ref,
    dkv_ref,
    g_ref,
    gt_ref,
    qt_ref,
):
    block = pl.program_id(0)
    heads, rows, lanes = q_ref.shape
    width = heads * HD

    @pl.when(block == 0)
    def _():
        dkv_ref[...] = jnp.zeros_like(dkv_ref)

    dq_ref[...] = jnp.zeros_like(dq_ref)
    half_lane = lax.broadcasted_iota(jnp.int32, (rows, HD), 1)
    dout_all = unpack_heads(dout_ref[0].astype(F32))
    for head in range(heads):
        dout = dout_all[:, head * HD : (head + 1) * HD]
        sums = sum_ref[head]
        total = sums[:, HD : HD + 1]
        g_low = dout / total
        delta = -jnp.sum(dout * sums[:, :HD], axis=1, keepdims=True) / (total * total)
        high = delta.astype(BF16).astype(F32)
        middle = (delta - high).astype(BF16).astype(F32)
        tail = jnp.where(
            half_lane == 0,
            high,
            jnp.where(half_lane == 1, middle, jnp.where(half_lane == 2, delta - high - middle, 0.0)),
        )
        g_ext = jnp.concatenate([g_low, tail], axis=1)
        g_ref[head] = g_ext.astype(BF16)
        gt_ref[head] = jnp.transpose(g_ext)[:HD].astype(BF16)
        qt_ref[head] = jnp.transpose(q_ref[head].astype(F32))[:HD].astype(BF16)

    low = low_ref[block]

    def step(window, low, index, carry):
        start = pl.multiple_of(low + index * window, align)
        for head in range(heads):
            k_part = k_ref[head, pl.ds(start, window), :]
            v_part = v_ref[head, pl.ds(start, window), :]
            score = lax.dot_general(q_ref[head], k_part, BY_LANES, preferred_element_type=F32)
            slope = lax.dot_general(g_ref[head], v_part, BY_LANES, preferred_element_type=F32)
            expo = jnp.exp2(score)
            d_score = (expo * slope).astype(BF16)
            expo = expo.astype(BF16)
            dq_ref[head] += jnp.dot(d_score, k_part, preferred_element_type=F32)
            dkv_ref[head, :HD, pl.ds(start, window)] += jnp.dot(qt_ref[head], d_score, preferred_element_type=F32)
            dkv_ref[head, HD:, pl.ds(start, window)] += jnp.dot(gt_ref[head], expo, preferred_element_type=F32)
        return carry

    units = count_ref[block]
    many = lax.div(units, 4)
    rest = lax.rem(units, 4)
    lax.fori_loop(0, many, functools.partial(step, 4 * align, low), 0)
    low = low + many * 4 * align

    @pl.when(rest >= 2)
    def _():
        step(2 * align, low, 0, 0)

    @pl.when(lax.rem(rest, 2) == 1)
    def _():
        step(align, low + lax.div(rest, 2) * 2 * align, 0, 0)

    lane = lax.broadcasted_iota(jnp.int32, (rows, lanes), 1)

    def turn_back(value, turn):
        swapped = jnp.where(lane < HD // 2, pltpu.roll(value, lanes - HD // 2, 1), pltpu.roll(value, HD // 2, 1))
        sine = pltpu.roll(turn, HD, 1)
        sine = jnp.where(lane < HD // 2, sine, -sine)
        return (value * turn + swapped * sine)[:, :HD]

    here = turn_ref[pl.ds(pl.multiple_of(block * rows, rows), rows), :]
    for head in range(heads):
        turned = turn_back(dq_ref[head] * HD ** (-0.5), here)
        d_ref[block, :, head * HD : (head + 1) * HD] = turned.astype(BF16)

    @pl.when(block == pl.num_programs(0) - 1)
    def _():
        def finish(piece, carry):
            start = pl.multiple_of(piece * rows, rows)
            turn = turn_ref[pl.ds(start, rows), :]
            for head in range(heads):
                both = jnp.transpose(dkv_ref[head, :, pl.ds(start, rows)])
                at = width + head * HD
                d_ref[piece, :, at : at + HD] = (turn_back(both, turn) * LN2).astype(BF16)
                d_ref[piece, :, width + at : width + at + HD] = both[:, HD:].astype(BF16)
            return carry

        lax.fori_loop(0, d_ref.shape[0], finish, 0)


def attend_back_heads(bounds, q_ext, k_ext, v_ext, sums, dout, turn, align=128):
    heads, length, lanes = q_ext.shape
    count_blocks = dout.shape[0]
    rows, width = length // count_blocks, heads * HD
    low, count = windows(bounds, length, align, align)
    whole = pl.BlockSpec((heads, length, lanes), lambda i, *_: (0, 0, 0))
    part = pl.BlockSpec((heads, rows, lanes), lambda i, *_: (0, i, 0))
    return pl.pallas_call(
        functools.partial(attend_back_kernel, align),
        out_shape=jax.ShapeDtypeStruct((count_blocks, rows, 3 * width), BF16),
        grid_spec=pltpu.PrefetchScalarGridSpec(
            num_scalar_prefetch=2,
            grid=(count_blocks,),
            in_specs=[
                part,
                part,
                pl.BlockSpec((1,) + dout.shape[1:], lambda i, *_: (i, 0, 0)),
                pl.BlockSpec((length, lanes), lambda i, *_: (0, 0)),
                whole,
                whole,
            ],
            out_specs=pl.BlockSpec((count_blocks, rows, 3 * width), lambda i, *_: (0, 0, 0)),
            scratch_shapes=[
                pltpu.VMEM((heads, rows, lanes), F32),
                pltpu.VMEM((heads, 2 * HD, length), F32),
                pltpu.VMEM((heads, rows, lanes), BF16),
                pltpu.VMEM((heads, HD, rows), BF16),
                pltpu.VMEM((heads, HD, rows), BF16),
            ],
        ),
        compiler_params=pltpu.CompilerParams(vmem_limit_bytes=VMEM_LIMIT),
        cost_estimate=pl.CostEstimate(
            flops=heads * length * length * 10 * lanes // 2,
            bytes_accessed=heads * length * lanes * 20,
            transcendentals=heads * length * length // 2,
        ),
        name="attend_back_heads",
    )(low, count, q_ext, sums, dout, turn, k_ext, v_ext)


def scatter_kernel(
    chunks,
    by_z,
    d_hbm,
    x_hbm,
    w_ref,
    dh_hbm,
    norm_ref,
    out_hbm,
    gw_all_ref,
    norm_out_ref,
    d_ref,
    x_ref,
    part_ref,
    gw_sum,
    gw_ref,
    dh_ref,
    out_ref,
    got_y,
    got_z,
    relay_y,
    relay_z,
    sent_y,
    sent_z,
    cross_out,
    cross_in,
    gw_got,
    gw_mine,
    gw_pair,
    gw_final,
    norm_got,
    norm_sent,
    send,
    recv,
    gw_send,
    gw_recv,
    norm_send,
    norm_recv,
    kept,
):
    me = lax.axis_index("seq")
    shard = lax.axis_index("shard")
    shards = gw_ref.shape[0]
    half = lax.div(me, GROUPS)
    y_near, z_near, partner = flip(me, 1), flip(me, 2), flip(me, 4)
    corner = flip(y_near, 2)
    barrier = pltpu.get_barrier_semaphore()
    for n in range(1, SEQ_SIZE):
        pl.semaphore_signal(
            barrier, inc=1, device_id={"seq": lax.rem(me + n, SEQ_SIZE)}, device_id_type=BY_MESH
        )
    for step in range(1, shards):
        pl.semaphore_signal(
            barrier, inc=1, device_id={"shard": lax.rem(shard + step, shards)}, device_id_type=BY_MESH
        )
    pl.semaphore_wait(barrier, SEQ_SIZE + shards - 2)

    started = []

    def go(source, target, sends, receives, slot, where):
        copy = pltpu.make_async_remote_copy(
            src_ref=source,
            dst_ref=target,
            send_sem=sends.at[slot],
            recv_sem=receives.at[slot],
            device_id=where,
            device_id_type=BY_MESH,
        )
        copy.start()
        started.append(copy)
        return copy

    rows = part_ref.shape[1] // chunks

    def band(chunk):
        return pl.ds(chunk * rows, rows)

    def piece(device, far):
        return flip(device, 4) if far else device

    def slot(kind, far, chunk):
        return (kind * 2 + (0 if far else 1)) * chunks + chunk

    def other(mask):
        index = 0
        for bit in (1, 2, 4):
            here, there = lax.rem(lax.div(me, bit), 2), lax.rem(lax.div(mask, bit), 2)
            index = index + bit * (here + there - 2 * here * there)
        return index

    masks = (7, 6, 5, 3, 2, 1, 4, 0)

    def fetch(mask, place):
        return pltpu.make_async_copy(d_hbm.at[other(mask)], d_ref.at[other(mask)], kept.at[8 + place])

    for place, mask in enumerate(masks):
        fetch(mask, place).start()
    loads = [
        pltpu.make_async_copy(dh_hbm, dh_ref, kept.at[4]),
        pltpu.make_async_copy(x_hbm, x_ref, kept.at[5]),
    ]
    for copy in loads:
        copy.start()

    def project(count, first, place):
        def body(n, carry):
            mask = first(n)
            fetch(mask, place + n).wait()
            index = other(mask)
            part_ref[index] = lax.dot_general(
                d_ref[index], w_ref[...], BY_LANES, preferred_element_type=F32
            ).astype(BF16)
            return carry

        lax.fori_loop(0, count, body, 0)

    norm_seq = [
        go(norm_ref, norm_got.at[n], norm_send, norm_recv, n, {"seq": lax.rem(me + n + 1, SEQ_SIZE)})
        for n in range(SEQ_SIZE - 1)
    ]

    from_corner, direct = {}, {}

    def send_pieces(far):
        for chunk in range(chunks):
            over_z = chunk < by_z
            from_corner[far, chunk] = go(
                part_ref.at[piece(corner, far), band(chunk)],
                (relay_y if over_z else relay_z).at[0 if far else 1, chunk if over_z else chunk - by_z],
                send,
                recv,
                slot(0, far, chunk),
                {"seq": y_near if over_z else z_near},
            )
        for chunk in range(chunks):
            over_z = chunk < by_z
            direct[far, chunk] = go(
                part_ref.at[piece(y_near if over_z else z_near, far), band(chunk)],
                (got_y if over_z else got_z).at[0 if far else 1, band(chunk)],
                send,
                recv,
                slot(1 if over_z else 2, far, chunk),
                {"seq": y_near if over_z else z_near},
            )

    project(3, lambda n: 7 - n, 0)
    send_pieces(True)
    project(3, lambda n: 3 - n, 3)
    project(2, lambda n: 4 - 4 * n, 6)
    relayed = {}

    def relay(far, chunk):
        over_z = chunk < by_z
        target = z_near if over_z else y_near
        index = chunk if over_z else chunk - by_z
        which = 0 if far else 1
        from_corner[far, chunk].wait_recv()
        source = relay_y if over_z else relay_z
        buffer = sent_y if over_z else sent_z
        passed = part_ref[piece(target, far), band(chunk)].astype(F32)
        buffer[which, index] = (source[which, index].astype(F32) + passed).astype(BF16)
        relayed[far, chunk] = go(
            buffer.at[which, index],
            (got_z if over_z else got_y).at[which, band(chunk)],
            send,
            recv,
            slot(2 if over_z else 1, far, chunk),
            {"seq": target},
        )

    def total(far, chunk):
        which = 0 if far else 1
        direct[far, chunk].wait_recv()
        relayed[far, chunk].wait_recv()
        return part_ref[piece(me, far), band(chunk)].astype(F32) + got_y[which, band(chunk)].astype(F32) + got_z[which, band(chunk)].astype(F32)

    for chunk in range(chunks):
        relay(True, chunk)
    send_pieces(False)
    for copy in loads:
        copy.wait()
    gw_sum[...] = jnp.zeros_like(gw_sum)

    def grow(n, carry):
        gw_sum[...] += lax.dot_general(
            x_ref[n], d_ref[n], (((0,), (0,)), ((), ())), preferred_element_type=F32
        )
        return carry

    lax.fori_loop(0, d_ref.shape[0], grow, 0)
    depth = gw_ref.shape[1]
    for owner in range(shards):
        gw_ref[owner] = gw_sum[owner * depth : (owner + 1) * depth, :].astype(BF16)
    gw_one = [
        go(
            gw_ref.at[lax.rem(shard + step, shards)],
            gw_got.at[step - 1],
            gw_send,
            gw_recv,
            step - 1,
            {"shard": lax.rem(shard + step, shards)},
        )
        for step in range(1, shards)
    ]
    norm_total = norm_ref[...]
    for n, copy in enumerate(norm_seq):
        copy.wait_recv()
        norm_total = norm_total + norm_got[n]
    norm_sent[...] = norm_total
    for copy in gw_one:
        copy.wait_recv()
    summed = gw_ref[shard].astype(F32)
    for step in range(1, shards):
        summed = summed + gw_got[step - 1].astype(F32)
    gw_mine[...] = summed.astype(BF16)
    gw_two = go(gw_mine, gw_pair, gw_send, gw_recv, shards - 1, {"seq": partner})
    norm_shard = [
        go(
            norm_sent,
            norm_got.at[SEQ_SIZE - 2 + step],
            norm_send,
            norm_recv,
            SEQ_SIZE - 2 + step,
            {"shard": lax.rem(shard + step, shards)},
        )
        for step in range(1, shards)
    ]
    crossing = []
    for chunk in range(chunks):
        cross_out[band(chunk)] = total(True, chunk).astype(BF16)
        crossing.append(
            go(cross_out.at[band(chunk)], cross_in.at[band(chunk)], send, recv, slot(3, True, chunk), {"seq": partner})
        )
    for chunk in range(chunks):
        relay(False, chunk)
    gw_two.wait_recv()
    gw_final[...] = (gw_mine[...].astype(F32) + gw_pair[...].astype(F32)).astype(BF16)
    group = lax.rem(me, GROUPS)
    gw_three = [
        go(gw_final, gw_all_ref.at[group], gw_send, gw_recv, shards + n, {"seq": device})
        for n, device in enumerate((y_near, z_near, corner))
    ]
    keep = pltpu.make_async_copy(gw_final, gw_all_ref.at[group], kept.at[0])
    keep.start()
    for chunk in range(chunks):
        out_ref[0, band(chunk)] = (total(False, chunk) + dh_ref[half, band(chunk)]).astype(BF16)
    out_near = pltpu.make_async_copy(out_ref.at[0], out_hbm.at[half], kept.at[2])
    out_near.start()
    norm_total = norm_sent[...]
    for step, copy in enumerate(norm_shard):
        copy.wait_recv()
        norm_total = norm_total + norm_got[SEQ_SIZE - 1 + step]
    norm_out_ref[...] = norm_total
    for chunk in range(chunks):
        crossing[chunk].wait_recv()
        other = 1 - half
        out_ref[1, band(chunk)] = (cross_in[band(chunk)].astype(F32) + dh_ref[other, band(chunk)]).astype(BF16)
    out_far = pltpu.make_async_copy(out_ref.at[1], out_hbm.at[1 - half], kept.at[3])
    out_far.start()
    for copy in gw_three:
        copy.wait_recv()
    keep.wait()
    out_near.wait()
    out_far.wait()
    for copy in started:
        copy.wait_send()


def scatter_gradients(d_heads, pieces, w_own, dh_one, norms, shards, chunks=4, by_z=3):
    _, rows, width = pieces.shape
    columns = d_heads.shape[2]
    depth = width // shards
    part = rows // chunks
    hbm = pl.BlockSpec(memory_space=pltpu.HBM)
    vmem = pl.BlockSpec(memory_space=pltpu.VMEM)
    dma = pltpu.SemaphoreType.DMA
    return pl.pallas_call(
        functools.partial(scatter_kernel, chunks, by_z),
        out_shape=(
            jax.ShapeDtypeStruct(dh_one.shape, BF16),
            jax.ShapeDtypeStruct((GROUPS, depth, columns), BF16),
            jax.ShapeDtypeStruct(norms.shape, F32),
        ),
        in_specs=[hbm, hbm, vmem, hbm, vmem],
        out_specs=(hbm, vmem, vmem),
        scratch_shapes=[
            pltpu.VMEM(d_heads.shape, BF16),
            pltpu.VMEM(pieces.shape, BF16),
            pltpu.VMEM(pieces.shape, BF16),
            pltpu.VMEM((width, columns), F32),
            pltpu.VMEM((shards, depth, columns), BF16),
            pltpu.VMEM(dh_one.shape, F32),
            pltpu.VMEM((2, rows, width), BF16),
            pltpu.VMEM((2, rows, width), BF16),
            pltpu.VMEM((2, rows, width), BF16),
            pltpu.VMEM((2, by_z, part, width), BF16),
            pltpu.VMEM((2, chunks - by_z, part, width), BF16),
            pltpu.VMEM((2, by_z, part, width), BF16),
            pltpu.VMEM((2, chunks - by_z, part, width), BF16),
            pltpu.VMEM((rows, width), BF16),
            pltpu.VMEM((rows, width), BF16),
            pltpu.VMEM((shards - 1, depth, columns), BF16),
            pltpu.VMEM((depth, columns), BF16),
            pltpu.VMEM((depth, columns), BF16),
            pltpu.VMEM((depth, columns), BF16),
            pltpu.VMEM((SEQ_SIZE + shards - 2,) + norms.shape, F32),
            pltpu.VMEM(norms.shape, F32),
            dma((7 * chunks,)),
            dma((7 * chunks,)),
            dma((shards + 3,)),
            dma((shards + 3,)),
            dma((SEQ_SIZE + shards - 2,)),
            dma((SEQ_SIZE + shards - 2,)),
            dma((8 + SEQ_SIZE,)),
        ],
        compiler_params=pltpu.CompilerParams(
            collective_id=2, has_side_effects=True, vmem_limit_bytes=VMEM_LIMIT
        ),
        cost_estimate=pl.CostEstimate(flops=60 * 10**9, bytes_accessed=64 * 2**20, transcendentals=0),
        name="scatter_gradients",
    )(d_heads, pieces, w_own, dh_one, norms)


def padded_rows(blocks, depth):
    return pl.cdiv((3 * blocks + 1) * depth, SEQ_SIZE * 16) * SEQ_SIZE * 16


def feed_forward_kernel(
    tokens_ref,
    joined_ref,
    cot_ref,
    out_hbm,
    gate_hbm,
    up_hbm,
    down_hbm,
    norms_ref,
    output_ref,
    dout_ref,
    dh_ref,
    norm_sums_ref,
    packed_ref,
    w_out,
    w_gate,
    w_up,
    w_down,
    flow,
    hat_one,
    inverse_one,
    x_low,
    x_turned,
    dm_low,
    gate_kept,
    up_kept,
    d_both,
    hidden_kept,
    staged,
    loads,
    stores,
):
    seqs, rows, width = dh_ref.shape
    shards = packed_ref.shape[0]
    depth = width // shards
    blocks = gate_hbm.shape[1] // width
    weights = ((out_hbm, w_out), (gate_hbm, w_gate), (up_hbm, w_up), (down_hbm, w_down))
    fetch = [pltpu.make_async_copy(src, dst, loads.at[n]) for n, (src, dst) in enumerate(weights)]
    tokens_in = pltpu.make_async_copy(tokens_ref, flow, loads.at[4])
    tokens_in.start()
    for copy in fetch:
        copy.start()
    gain_one, bias_one, gain_two, bias_two = (norms_ref[n : n + 1, :] for n in range(4))

    def mean(value):
        return jnp.sum(value, axis=-1, keepdims=True) * (1.0 / width)

    def rows_of(seq):
        return pl.ds(pl.multiple_of(seq * rows, rows), rows)

    fetch[0].wait()
    tokens_in.wait()

    def enter(seq, carry):
        h_one = flow[seq].astype(F32)
        for group in range(GROUPS):
            h_one = h_one + jnp.dot(
                unpack_heads(joined_ref[seq * GROUPS + group]),
                w_out[group * depth : (group + 1) * depth, :],
                preferred_element_type=F32,
            )
        centered = h_one - mean(h_one)
        inverse = lax.rsqrt(mean(centered * centered) + EPS)
        normed = centered * inverse
        hat_one[seq] = normed
        inverse_one[seq] = inverse
        x_one = normed * gain_one + bias_one
        dh_ref[seq] = x_one
        x_low[seq] = x_one.astype(BF16)
        x_turned[:, rows_of(seq)] = jnp.transpose(x_one).astype(BF16)
        return carry

    lax.fori_loop(0, seqs, enter, 0)
    cot_in = pltpu.make_async_copy(cot_ref, flow, loads.at[4])
    cot_in.start()
    for copy in fetch[1:]:
        copy.wait()

    def forward(step, carry):
        block, seq = lax.div(step, seqs), lax.rem(step, seqs)
        at = pl.ds(pl.multiple_of(block * width, width), width)
        gate = jnp.dot(x_low[seq], w_gate[:, at], preferred_element_type=F32)
        up = jnp.dot(x_low[seq], w_up[:, at], preferred_element_type=F32)
        gate_kept[block, seq] = gate.astype(gate_kept.dtype)
        up_kept[block, seq] = up.astype(up_kept.dtype)
        hidden = (gate * jax.nn.sigmoid(gate) * up).astype(BF16)
        dh_ref[seq] += jnp.dot(hidden, w_down[at, :], preferred_element_type=F32)
        return carry

    lax.fori_loop(0, blocks * seqs, forward, 0)

    cot_in.wait()
    def turn(seq, carry):
        gain_two_sum, bias_two_sum = carry
        h_two = dh_ref[seq]
        centered = h_two - mean(h_two)
        inverse = lax.rsqrt(mean(centered * centered) + EPS)
        normed = centered * inverse
        cot = flow[seq].astype(F32)
        flow[seq] = (normed * gain_two + bias_two).astype(BF16)
        gain_two_sum = gain_two_sum + jnp.sum(cot * normed, axis=0, keepdims=True)
        bias_two_sum = bias_two_sum + jnp.sum(cot, axis=0, keepdims=True)
        scaled = cot * gain_two
        dh_two = inverse * (scaled - mean(scaled) - normed * mean(scaled * normed))
        dh_ref[seq] = dh_two
        dm_low[rows_of(seq), :] = dh_two.astype(BF16)
        return gain_two_sum, bias_two_sum

    empty = jnp.zeros((1, width), F32)
    gain_two_sum, bias_two_sum = lax.fori_loop(0, seqs, turn, (empty, empty))
    output_out = pltpu.make_async_copy(flow, output_ref, loads.at[4])
    output_out.start()

    def store(kind, block):
        if kind < 2:
            start = pl.multiple_of((kind * blocks + block) * depth, depth)
            return [
                pltpu.make_async_copy(
                    staged.at[kind, pl.ds(shard * depth, depth)],
                    packed_ref.at[shard, pl.ds(start, depth)],
                    stores.at[kind, shard],
                )
                for shard in range(shards)
            ]
        start = 2 * blocks * depth
        return [
            pltpu.make_async_copy(
                staged.at[2], packed_ref.at[block, pl.ds(start, width)], stores.at[2, 0]
            )
        ]

    def backward(block, carry):
        at = pl.ds(pl.multiple_of(block * width, width), width)
        def rows_back(seq, carry):
            here = rows_of(seq)
            d_hidden = lax.dot_general(dm_low[here, :], w_down[at, :], BY_LANES, preferred_element_type=F32)
            gate = gate_kept[block, seq].astype(F32)
            up = up_kept[block, seq].astype(F32)
            sigma = jax.nn.sigmoid(gate)
            smooth = gate * sigma
            hidden_kept[here, :] = (smooth * up).astype(BF16)
            dg = (d_hidden * up * (sigma + smooth * (1.0 - sigma))).astype(BF16)
            du = (d_hidden * smooth).astype(BF16)
            d_both[0, here, :] = dg
            d_both[1, here, :] = du
            dh_ref[seq] += lax.dot_general(dg, w_gate[:, at], BY_LANES, preferred_element_type=F32)
            dh_ref[seq] += lax.dot_general(du, w_up[:, at], BY_LANES, preferred_element_type=F32)
            return carry

        lax.fori_loop(0, seqs, rows_back, 0)

        @pl.when(block > 0)
        def _():
            for kind in range(3):
                for copy in store(kind, block - 1):
                    copy.wait()

        def grow(kind, carry):
            staged[kind] = jnp.dot(x_turned[...], d_both[kind], preferred_element_type=F32).astype(BF16)
            return carry

        lax.fori_loop(0, 2, grow, 0)
        staged[2] = lax.dot_general(
            hidden_kept[...], dm_low[...], (((0,), (0,)), ((), ())), preferred_element_type=F32
        ).astype(BF16)
        for kind in range(3):
            for copy in store(kind, block):
                copy.start()
        return carry

    lax.fori_loop(0, blocks, backward, 0)

    def leave(seq, carry):
        gain_one_sum, bias_one_sum = carry
        dx_one = dh_ref[seq]
        normed = hat_one[seq]
        gain_one_sum = gain_one_sum + jnp.sum(dx_one * normed, axis=0, keepdims=True)
        bias_one_sum = bias_one_sum + jnp.sum(dx_one, axis=0, keepdims=True)
        scaled = dx_one * gain_one
        dh_one = inverse_one[seq] * (scaled - mean(scaled) - normed * mean(scaled * normed))
        dh_ref[seq] = dh_one
        d_attn = dh_one.astype(BF16)
        d_both[0, rows_of(seq), :] = d_attn
        for group in range(GROUPS):
            dout = lax.dot_general(
                d_attn, w_out[group * depth : (group + 1) * depth, :], BY_LANES, preferred_element_type=F32
            )
            first, last = pack_heads(dout)
            dout_ref[seq * GROUPS + group, :rows] = first.astype(BF16)
            dout_ref[seq * GROUPS + group, rows:] = last.astype(BF16)
        return gain_one_sum, bias_one_sum

    gain_one_sum, bias_one_sum = lax.fori_loop(0, seqs, leave, (empty, empty))
    for kind in range(3):
        for copy in store(kind, blocks - 1):
            copy.wait()
    def grow_out(group, carry):
        grad = jnp.zeros((depth, width), F32)
        for seq in range(seqs):
            grad = grad + lax.dot_general(
                unpack_heads(joined_ref[seq * GROUPS + group]),
                d_both[0, seq * rows : (seq + 1) * rows, :],
                (((0,), (0,)), ((), ())),
                preferred_element_type=F32,
            )
        staged[0, pl.ds(pl.multiple_of(group * depth, depth), depth), :] = grad.astype(BF16)
        return carry

    lax.fori_loop(0, GROUPS, grow_out, 0)
    last = [
        pltpu.make_async_copy(
            staged.at[0, pl.ds(shard * depth, depth)],
            packed_ref.at[shard, pl.ds(3 * blocks * depth, depth)],
            stores.at[0, shard],
        )
        for shard in range(shards)
    ]
    used = (3 * blocks + 1) * depth
    rest = packed_ref.shape[1] - used
    staged[1, :rest, :] = jnp.zeros((rest, width), BF16)
    last += [
        pltpu.make_async_copy(
            staged.at[1, pl.ds(0, rest)], packed_ref.at[shard, pl.ds(used, rest)], stores.at[1, shard]
        )
        for shard in range(shards)
    ]
    for copy in last:
        copy.start()
    norm_sums_ref[0:1, :] = gain_one_sum
    norm_sums_ref[1:2, :] = bias_one_sum
    norm_sums_ref[2:3, :] = gain_two_sum
    norm_sums_ref[3:4, :] = bias_two_sum
    for copy in last:
        copy.wait()
    output_out.wait()


def feed_forward(tokens, joined, cotangent, w_out, w_gate, w_up, w_down, norms, kept=BF16):
    seqs, rows, width = tokens.shape
    total = seqs * rows
    hidden = w_gate.shape[1]
    blocks = hidden // width
    depth = width // GROUPS
    vmem = pl.BlockSpec(memory_space=pltpu.VMEM)
    hbm = pl.BlockSpec(memory_space=pltpu.HBM)
    dma = pltpu.SemaphoreType.DMA
    return pl.pallas_call(
        feed_forward_kernel,
        out_shape=(
            jax.ShapeDtypeStruct(tokens.shape, BF16),
            jax.ShapeDtypeStruct(joined.shape, BF16),
            jax.ShapeDtypeStruct(tokens.shape, F32),
            jax.ShapeDtypeStruct((4, width), F32),
            jax.ShapeDtypeStruct((GROUPS, padded_rows(blocks, depth), width), BF16),
        ),
        in_specs=[hbm, vmem, hbm, hbm, hbm, hbm, hbm, vmem],
        out_specs=(hbm, vmem, vmem, vmem, hbm),
        scratch_shapes=[
            pltpu.VMEM(w_out.shape, BF16),
            pltpu.VMEM(w_gate.shape, BF16),
            pltpu.VMEM(w_up.shape, BF16),
            pltpu.VMEM(w_down.shape, BF16),
            pltpu.VMEM(tokens.shape, BF16),
            pltpu.VMEM(tokens.shape, F32),
            pltpu.VMEM((seqs, rows, 1), F32),
            pltpu.VMEM(tokens.shape, BF16),
            pltpu.VMEM((width, total), BF16),
            pltpu.VMEM((total, width), BF16),
            pltpu.VMEM((blocks, seqs, rows, width), kept),
            pltpu.VMEM((blocks, seqs, rows, width), kept),
            pltpu.VMEM((2, total, width), BF16),
            pltpu.VMEM((total, width), BF16),
            pltpu.VMEM((3, width, width), BF16),
            dma((5,)),
            dma((3, GROUPS)),
        ],
        compiler_params=pltpu.CompilerParams(vmem_limit_bytes=FEED_LIMIT),
        cost_estimate=pl.CostEstimate(
            flops=6 * total * width * (3 * hidden + width),
            bytes_accessed=2 * 2 * (3 * hidden + width) * width + 20 * total * width,
            transcendentals=2 * total * hidden,
        ),
        name="feed_forward",
    )(tokens, joined, cotangent, w_out, w_gate, w_up, w_down, norms)


def gather_rows_kernel(chunks, by_z, own_ref, rows_ref, send, recv, kept):
    me = lax.axis_index("seq")
    y_near, z_near, partner = flip(me, 1), flip(me, 2), flip(me, 4)
    barrier = pltpu.get_barrier_semaphore()
    for device in (y_near, z_near, partner):
        pl.semaphore_signal(barrier, inc=1, device_id={"seq": device}, device_id_type=BY_MESH)
    pl.semaphore_wait(barrier, 3)
    count = own_ref.shape[0]
    part = count // chunks
    started = []

    def go(source, target, slot, device):
        copy = pltpu.make_async_remote_copy(
            src_ref=source,
            dst_ref=target,
            send_sem=send.at[slot],
            recv_sem=recv.at[slot],
            device_id={"seq": device},
            device_id_type=BY_MESH,
        )
        copy.start()
        started.append(copy)
        return copy

    def band(device, chunk):
        return rows_ref.at[pl.ds(device * count + chunk * part, part)]

    def own(chunk, slot, device):
        return go(own_ref.at[pl.ds(chunk * part, part)], band(me, chunk), slot * chunks + chunk, device)

    def relay(device, chunk, slot, target):
        return go(band(device, chunk), band(device, chunk), slot * chunks + chunk, target)

    crossing = [own(chunk, 0, partner) for chunk in range(chunks)]
    own_y, own_z = [], []
    for chunk in range(chunks):
        own_y.append(own(chunk, 1, y_near))
        own_z.append(own(chunk, 2, z_near))
    keep = pltpu.make_async_copy(own_ref, rows_ref.at[pl.ds(me * count, count)], kept)
    keep.start()
    cross_y, cross_z, corner = [], [], []
    for chunk in range(chunks):
        own_y[chunk].wait_recv()
        if chunk < by_z:
            corner.append(relay(y_near, chunk, 5, z_near))
        own_z[chunk].wait_recv()
        if chunk >= by_z:
            corner.append(relay(z_near, chunk, 5, y_near))
        crossing[chunk].wait_recv()
        cross_y.append(relay(partner, chunk, 3, y_near))
        cross_z.append(relay(partner, chunk, 4, z_near))
    for chunk in range(chunks):
        cross_y[chunk].wait_recv()
        if chunk < by_z:
            corner.append(relay(flip(y_near, 4), chunk, 6, z_near))
        cross_z[chunk].wait_recv()
        if chunk >= by_z:
            corner.append(relay(flip(z_near, 4), chunk, 6, y_near))
    for copy in corner:
        copy.wait_recv()
    keep.wait()
    for copy in started:
        copy.wait_send()


def gather_rows(owned, chunks=8, by_z=3):
    hbm = pl.BlockSpec(memory_space=pltpu.HBM)
    dma = pltpu.SemaphoreType.DMA
    return pl.pallas_call(
        functools.partial(gather_rows_kernel, chunks, by_z),
        out_shape=jax.ShapeDtypeStruct((SEQ_SIZE * owned.shape[0], owned.shape[1]), BF16),
        in_specs=[hbm],
        out_specs=hbm,
        scratch_shapes=[dma((7 * chunks,)), dma((7 * chunks,)), dma],
        compiler_params=pltpu.CompilerParams(collective_id=5, has_side_effects=True),
        name="gather_rows",
    )(owned)


def unpack_kernel(gate_rows, up_rows, down_rows, out_rows, columns, gate_ref, up_ref, down_ref, out_ref, qkv_ref):
    gate_ref[...] = gate_rows[...].astype(F32)
    up_ref[...] = up_rows[...].astype(F32)
    down_ref[...] = down_rows[...].astype(F32)

    @pl.when(pl.program_id(0) == 0)
    def _():
        out_ref[...] = out_rows[...].astype(F32)
        groups, _, width = columns.shape
        width = width // 3
        for group in range(groups):
            for part in range(3):
                at = (part * groups + group) * width
                qkv_ref[:, at : at + width] = columns[group, :, part * width : (part + 1) * width].astype(F32)


def unpack_gradients(rows, columns, blocks):
    groups, depth, thirds = columns.shape
    width = rows.shape[1]
    piece = [
        pl.BlockSpec((depth, width), lambda i, first=first, step=step: (first + step * i, 0))
        for first, step in ((0, 1), (blocks, 1), (2 * blocks, 1), (3 * blocks, 0))
    ]
    return pl.pallas_call(
        unpack_kernel,
        out_shape=(
            jax.ShapeDtypeStruct((depth, blocks * width), F32),
            jax.ShapeDtypeStruct((depth, blocks * width), F32),
            jax.ShapeDtypeStruct((blocks * depth, width), F32),
            jax.ShapeDtypeStruct((depth, width), F32),
            jax.ShapeDtypeStruct((depth, groups * thirds), F32),
        ),
        grid=(blocks,),
        in_specs=piece + [pl.BlockSpec(columns.shape, lambda i: (0, 0, 0))],
        out_specs=(
            pl.BlockSpec((depth, width), lambda i: (0, i)),
            pl.BlockSpec((depth, width), lambda i: (0, i)),
            pl.BlockSpec((depth, width), lambda i: (i, 0)),
            pl.BlockSpec((depth, width), lambda i: (0, 0)),
            pl.BlockSpec((depth, groups * thirds), lambda i: (0, 0)),
        ),
        name="unpack_gradients",
    )(rows, rows, rows, rows, columns)


def document_places(seg_row):
    length = seg_row.shape[0]
    ids = jnp.arange(LANES - HD, dtype=jnp.int32)[:, None]
    starts = jnp.sum((seg_row[None, :] < ids).astype(jnp.int32), axis=1, keepdims=True)
    start = jnp.sum(jnp.where(seg_row[None, :] == ids, starts, 0), axis=0)
    return jnp.arange(length, dtype=jnp.int32) - start


def exchange_kernel(sent_ref, taken_ref, send, recv, kept):
    me = lax.axis_index("seq")
    barrier = pltpu.get_barrier_semaphore()
    others = [lax.rem(me + step, SEQ_SIZE) for step in range(1, SEQ_SIZE)]
    for device in others:
        pl.semaphore_signal(barrier, inc=1, device_id={"seq": device}, device_id_type=BY_MESH)
    pl.semaphore_wait(barrier, SEQ_SIZE - 1)
    copies = []
    for step, device in enumerate(others):
        copy = pltpu.make_async_remote_copy(
            src_ref=sent_ref.at[device],
            dst_ref=taken_ref.at[me],
            send_sem=send.at[step],
            recv_sem=recv.at[step],
            device_id={"seq": device},
            device_id_type=BY_MESH,
        )
        copy.start()
        copies.append(copy)
    keep = pltpu.make_async_copy(sent_ref.at[me], taken_ref.at[me], kept)
    keep.start()
    keep.wait()
    for copy in copies:
        copy.wait()


def exchange(blocks, collective_id):
    hbm = pl.BlockSpec(memory_space=pltpu.HBM)
    dma = pltpu.SemaphoreType.DMA
    return pl.pallas_call(
        exchange_kernel,
        out_shape=jax.ShapeDtypeStruct(blocks.shape, blocks.dtype),
        in_specs=[hbm],
        out_specs=hbm,
        scratch_shapes=[dma((SEQ_SIZE - 1,)), dma((SEQ_SIZE - 1,)), dma],
        compiler_params=pltpu.CompilerParams(collective_id=collective_id, has_side_effects=True),
        name="exchange",
    )(blocks)


def head_columns(w_qkv, group, held):
    depth = w_qkv.shape[0]
    split = w_qkv.reshape(depth, 3, GROUPS, held, HD)
    mine = lax.dynamic_index_in_dim(split, group, 2, keepdims=False)
    second = mine * jnp.array([1, 1, 0], w_qkv.dtype)[None, :, None, None]
    return jnp.concatenate([mine, second], axis=-1).reshape(depth, 3 * held * 2 * HD)


def local_heads(
    shards,
    tokens,
    segments,
    positions,
    cotangent,
    w_qkv,
    w_out,
    w_gate,
    w_up,
    w_down,
    ln1_gain,
    ln1_bias,
    ln2_gain,
    ln2_bias,
):
    seq_count, row_count, model_width = tokens.shape
    held = HEADS // GROUPS
    length = row_count * SEQ_SIZE
    me = lax.axis_index("seq")
    seg_row = lax.dynamic_index_in_dim(segments, me // GROUPS, 0, keepdims=False)

    def gather(shard):
        return lax.all_gather(shard, "shard", axis=0, tiled=True)

    freqs = jnp.exp(jnp.arange(HD // 2, dtype=F32) * (-math.log(ROPE_BASE) / (HD // 2)))
    freq = jnp.tile(freqs, LANES // (HD // 2))[None]
    place = document_places(seg_row).astype(F32).reshape(SEQ_SIZE, 1, row_count)
    norm_rows = jnp.stack([ln1_gain, ln1_bias, ln2_gain, ln2_bias]).astype(F32)
    pieces, w_heads, norms, turn = gather_tokens(
        tokens, head_columns(w_qkv, me % GROUPS, held), norm_rows, place, freq, shards
    )
    norms = jnp.transpose(norms, (1, 0, 2)).reshape(4, model_width)
    full_out, full_gate, full_up, full_down = (gather(w) for w in (w_out, w_gate, w_up, w_down))
    bounds = document_bounds(seg_row, row_count)
    q_ext, k_ext, v_ext = project_heads(
        seg_row.astype(F32), turn, pieces, w_heads.reshape(model_width, -1), held
    )
    sums, joined_own = attend_heads(bounds, q_ext, k_ext, v_ext, row_count)
    output, d_joined, dh_one, norms_part, packed = feed_forward(
        tokens, exchange(joined_own, 3), cotangent, full_out, full_gate, full_up, full_down, norms
    )
    depth = model_width // shards
    ff_blocks = full_gate.shape[1] // model_width
    owned = lax.psum_scatter(
        packed.reshape(-1, model_width), ("shard", "seq"), scatter_dimension=0, tiled=True
    )

    dout = exchange(d_joined, 4)
    d_heads = attend_back_heads(bounds, q_ext, k_ext, v_ext, sums, dout, turn)
    w_lanes = w_heads.reshape(model_width, -1)
    w_own = jnp.concatenate(
        [w_lanes[:, at : at + HD] for at in range(0, w_lanes.shape[1], LANES)], axis=1
    )
    input_grad, columns, norm_sums = scatter_gradients(d_heads, pieces, w_own, dh_one, norms_part, shards)
    columns, owned = lax.optimization_barrier((columns, owned))
    shared = gather_rows(owned)
    grad_gate, grad_up, grad_down, grad_out, grad_qkv = unpack_gradients(shared, columns, ff_blocks)
    shard = lax.axis_index("shard")
    norm_sums = lax.dynamic_slice_in_dim(norm_sums, shard * depth, depth, 1)
    return (
        output,
        input_grad,
        grad_qkv,
        grad_out,
        grad_gate,
        grad_up,
        grad_down,
        norm_sums[0],
        norm_sums[1],
        norm_sums[2],
        norm_sums[3],
    )


def solution(mesh):
    in_specs = (
        P("shard", "seq", None),
        P("shard", None),
        P("shard", "seq"),
        P("shard", "seq", None),
        P("shard", None),
        P("shard", None),
        P("shard", None),
        P("shard", None),
        P("shard", None),
        P("shard"),
        P("shard"),
        P("shard"),
        P("shard"),
    )
    out_specs = (
        P("shard", "seq", None),
        P("shard", "seq", None),
        P("shard", None),
        P("shard", None),
        P("shard", None),
        P("shard", None),
        P("shard", None),
        P("shard"),
        P("shard"),
        P("shard"),
        P("shard"),
    )
    body = functools.partial(local_heads, mesh.shape["shard"]) if (mesh.shape["seq"], mesh.shape["shard"]) == (SEQ_SIZE, GROUPS) else local
    return jax.shard_map(body, mesh=mesh, in_specs=in_specs, out_specs=out_specs, check_vma=False)
```

profile of v0, /device:TPU:20, one launch (start us, length us, event | category | flops | bytes accessed | tf_op | source)
XLA Modules:
  0.0 551.1 jit_solution(557455448480040716)
XLA Ops:
  7.2 0.0 all-gather.5.cloned.1.call-start
  7.2 0.7 all-gather.5.cloned.1.call-update
  7.9 0.0 copy-start.4
  7.9 0.0 copy-start.2
  7.9 0.0 all-gather.11.cloned.1.call-start
  8.0 0.7 all-gather.11.cloned.1.call-update
  8.7 0.0 all-gather.7.cloned.1.call-start
  8.7 0.7 all-gather.7.cloned.1.call-update
  9.4 0.0 copy-start.5
  9.4 0.0 all-gather.9.cloned.1.call-start
  9.5 0.5 all-gather.9.cloned.1.call-update
  10.0 0.0 reduce-scatter.2.cloned.1.call-start
  10.1 0.0 copy-done.4
  10.1 0.6 fusion.2
  10.7 0.1 slice.45
  10.8 0.1 slice.46
  10.9 0.0 copy-done.2
  10.9 0.6 copy.30
  11.5 0.0 copy-start.6
  11.5 0.0 copy-start.7
  11.5 0.0 copy-start.8
  11.5 0.0 copy-start.9
  11.6 0.0 copy-done.5
  11.6 0.1 broadcast_multiply_fusion
  11.7 0.1 pad_maximum_fusion
  11.8 1.0 copy.33.w_ref
  12.8 0.0 copy-done.6
  12.8 0.0 copy-done.7
  12.8 0.0 copy-done.8
  12.8 0.0 copy-done.9
  12.9 0.6 broadcast_in_dim_tile.3.freq_ref
  13.4 0.6 maximum_convert_fusion.n_ref
  14.0 0.2 convert_reduce_fusion
  14.3 0.2 select_reduce_fusion
  14.5 0.6 subtract_convert_fusion.place_ref
  15.1 70.9 %gather_tokens.1 = (bf16[8,512,768]{2,1,0:T(8,128)(2,1)}, bf16[4,192,1152]{2,1,0:T(8,128)(2,1)}, f32[4,4,192]{2,1,0:T(4,128)}, f32[4096,128]{1,0:T(8,128)}) custom-call(bf16[2,512,768]{2,1,0:T(8,128)(2,1)} %tokens_ref.1, bf16[192,1152]{1,0:T(8,128)(2,1)} %copy.33.w_ref, f32[4,192]{1,0:T(4,128)} %maximum_convert_fusion.n_ref, ...), custom_call_target="tpu_custom_call" | custom-call | tf_op jit(solution)/shard_map/gather_tokens/pallas_call | solution.py:489
  86.1 0.2 convert_reduce_fusion.1
  86.3 0.5 subtract_minimum_fusion
  86.9 15.1 %project_heads.1 = (bf16[3,4096,128]{2,1,0:T(8,128)(2,1)}, bf16[3,4096,128]{2,1,0:T(8,128)(2,1)}, bf16[3,4096,128]{2,1,0:T(8,128)(2,1)}) custom-call(f32[8,1,512]{2,1,0:T(1,128)} %bitcast.26, f32[4096,128]{1,0:T(8,128)} %get-tuple-element.35.turn_ref, bf16[8,512,768]{2,1,0:T(8,128)(2,1)} %get-tuple-element.36.x_ref.x_hbm, bf16[768,1152]{1,0:T(8,128)(2,1)} %bitcast.18), custom_call_target="tpu_custom_call" | custom-call | flops 7247757312 | bytes 17825792 | tf_op jit(solution)/shard_map/project_heads/pallas_call | solution.py:547
  102.0 40.4 %attend_heads.1 = (f32[3,4096,128]{2,1,0:T(8,128)}, bf16[8,768,128]{2,1,0:T(8,128)(2,1)}) custom-call(s32[8]{0:T(128)} %get-tuple-element.82.low_ref, s32[8]{0:T(128)} %get-tuple-element.83.count_ref, bf16[3,4096,128]{2,1,0:T(8,128)(2,1)} %get-tuple-element.38.q_ref, bf16[3,4096,128]{2,1,0:T(8,128)(2,1)} %get-tuple-element.39.k_ref, ...), custom_call_target="tpu_custom_call" | custom-call | flops 12884901888 | bytes 15728640 | tf_op jit(solution)/shard_map/attend_heads/pallas_call | solution.py:610
  142.4 0.0 copy-start.3
  142.4 33.1 %exchange.2.joined_ref = bf16[8,768,128]{2,1,0:T(8,128)(2,1)} custom-call(bf16[8,768,128]{2,1,0:T(8,128)(2,1)} %get-tuple-element.41.sent_ref), custom_call_target="tpu_custom_call" | custom-call | tf_op jit(solution)/shard_map/exchange/pallas_call | solution.py:1551
  175.5 0.0 copy-done.3
  175.5 0.7 reshape.89.norms_ref
  176.2 0.0 all-gather.5.cloned.1.call-done.out_hbm
  176.2 0.0 all-gather.11.cloned.1.call-done.down_hbm
  176.2 0.0 all-gather.7.cloned.1.call-done.gate_hbm
  176.2 0.0 all-gather.9.cloned.1.call-done.up_hbm
  176.2 74.7 %feed_forward.1 = (bf16[2,512,768]{2,1,0:T(8,128)(2,1)}, bf16[8,768,128]{2,1,0:T(8,128)(2,1)}, f32[2,512,768]{2,1,0:T(8,128)}, f32[4,768]{1,0:T(4,128)}, bf16[4,2560,768]{2,1,0:T(8,128)(2,1)}) custom-call(bf16[2,512,768]{2,1,0:T(8,128)(2,1)} %tokens_ref.1, bf16[8,768,128]{2,1,0:T(8,128)(2,1)} %exchange.2.joined_ref, bf16[2,512,768]{2,1,0:T(8,128)(2,1)} %cot_ref.1, ...), custom_call_target="tpu_custom_call" | custom-call | flops 47110422528 | bytes 46399488 | tf_op jit(solution)/shard_map/feed_forward/pallas_call | solution.py:1350
  251.0 0.0 copy-start
  251.0 0.0 reduce-scatter.2.cloned.1.call-update
  251.0 1.4 copy-done
  252.4 0.3 fusion.3
  252.8 1.9 concatenate.7.w_ref
  254.7 36.8 %exchange.3.dout_ref = bf16[8,768,128]{2,1,0:T(8,128)(2,1)} custom-call(bf16[8,768,128]{2,1,0:T(8,128)(2,1)} %get-tuple-element.45.sent_ref), custom_call_target="tpu_custom_call" | custom-call | tf_op jit(solution)/shard_map/exchange/pallas_call | solution.py:1551
  291.5 97.7 %attend_back_heads.1.d_hbm = bf16[8,512,576]{2,1,0:T(8,128)(2,1)} custom-call(s32[8]{0:T(128)} %get-tuple-element.61.low_ref, s32[8]{0:T(128)} %get-tuple-element.62.count_ref, bf16[3,4096,128]{2,1,0:T(8,128)(2,1)} %get-tuple-element.38.q_ref, f32[3,4096,128]{2,1,0:T(8,128)} %get-tuple-element.44.sum_ref, bf16[8,768,128]{2,1,0:T(8,128)(2,1)} %exchange.3.dout_ref, ...), custom_call_target="tpu_custom_call" | custom-call | flops 32212254720 | bytes 31457280 | tf_op jit(solution)/shard_map/attend_back_heads/pallas_call | solution.py:744
  389.2 101.5 %scatter_gradients.1 = (bf16[2,512,768]{2,1,0:T(8,128)(2,1)}, bf16[4,192,576]{2,1,0:T(8,128)(2,1)}, f32[4,768]{1,0:T(4,128)}) custom-call(bf16[8,512,576]{2,1,0:T(8,128)(2,1)} %attend_back_heads.1.d_hbm, bf16[8,512,768]{2,1,0:T(8,128)(2,1)} %get-tuple-element.36.x_ref.x_hbm, bf16[768,576]{1,0:T(8,128)(2,1)} %concatenate.7.w_ref, ...), custom_call_target="tpu_custom_call" | custom-call | flops 60000002048 | bytes 67108864 | tf_op jit(solution)/shard_map/scatter_gradients/pallas_call | solution.py:1053
  490.7 1.5 fusion.4
  492.2 0.0 reduce-scatter.2.cloned.1.call-done.own_ref
  492.2 44.2 %gather_rows.1.gate_rows.up_rows.down_rows.out_rows = bf16[2560,768]{1,0:T(8,128)(2,1)} custom-call(bf16[320,768]{1,0:T(8,128)(2,1)} %reduce-scatter.2.cloned.1.call-done.own_ref), custom_call_target="tpu_custom_call" | custom-call | tf_op jit(solution)/shard_map/gather_rows/pallas_call | solution.py:1458
  536.5 0.0 copy-start.1
  536.5 6.9 %unpack_gradients.1 = (f32[192,3072]{1,0:T(8,128)}, f32[192,3072]{1,0:T(8,128)}, f32[768,768]{1,0:T(8,128)}, f32[192,768]{1,0:T(8,128)}, f32[192,2304]{1,0:T(8,128)}) custom-call(bf16[2560,768]{1,0:T(8,128)(2,1)} %gather_rows.1.gate_rows.up_rows.down_rows.out_rows, bf16[2560,768]{1,0:T(8,128)(2,1)} %gather_rows.1.gate_rows.up_rows.down_rows.out_rows, ...), custom_call_target="tpu_custom_call" | custom-call | tf_op jit(solution)/shard_map/unpack_gradients/pallas_call | solution.py:1492
  543.4 0.0 copy-done.1
  543.4 1.1 copy.35
  (8 shorter events, 0.1 us)
Async XLA Ops:
  7.2 169.1 %all-gather.5.cloned.1.call-start = ((), (), s32[]{:S(2)}) async-start(), calls=%async_computation.1 | async-start | bytes 1474560 | tf_op jit(solution)/shard_map/all_gather | solution.py:1593
  7.9 2.2 copy-start.4
  7.9 3.0 copy-start.2
  7.9 168.3 %all-gather.11.cloned.1.call-start = ((), (), s32[]{:S(2)}) async-start(), calls=%async_computation.4 | async-start | bytes 5898240 | tf_op jit(solution)/shard_map/all_gather | solution.py:1593
  8.7 167.6 %all-gather.7.cloned.1.call-start = ((), (), s32[]{:S(2)}) async-start(), calls=%async_computation.2 | async-start | bytes 5898240 | tf_op jit(solution)/shard_map/all_gather | solution.py:1593
  9.4 2.1 copy-start.5
  9.4 166.8 %all-gather.9.cloned.1.call-start = ((), (), s32[]{:S(2)}) async-start(), calls=%async_computation.3 | async-start | bytes 5898240 | tf_op jit(solution)/shard_map/all_gather | solution.py:1593
  10.0 482.2 %reduce-scatter.2.cloned.1.call-start = ((), (), s32[]{:S(2)}) async-start(), calls=%async_computation.5 | async-start | bytes 16220160 | tf_op jit(solution)/shard_map/reduce_scatter | solution.py:1614
  11.5 1.3 copy-start.6
  11.5 1.3 copy-start.7
  11.5 1.3 copy-start.8
  11.5 1.3 copy-start.9
  142.4 33.1 %copy-start.3 = (f32[4,4,192]{2,1,0:T(4,128)S(1)}, f32[4,4,192]{2,1,0:T(4,128)}, u32[]{:S(2)}) copy-start(f32[4,4,192]{2,1,0:T(4,128)} %get-tuple-element.42) | copy-start | bytes 36868
  251.0 1.5 copy-start
  536.5 6.9 %copy-start.1 = (bf16[2,512,768]{2,1,0:T(8,128)(2,1)S(1)}, bf16[2,512,768]{2,1,0:T(8,128)(2,1)}, u32[]{:S(2)}) copy-start(bf16[2,512,768]{2,1,0:T(8,128)(2,1)} %get-tuple-element.98) | copy-start | bytes 4718596
Sparse Core Ops, SparseCore 0:
  9.5 24.8 all-gather.4
  36.0 37.4 all-gather.10
  75.0 37.4 all-gather.6
  113.9 37.4 all-gather.8
  251.1 189.5 reduce-scatter.1
where the time goes:
time: 555 us; the launch traced here: 551 us
  Pallas kernels  521 us (94%)
  between operations  14.1 us (3%)
  local copies, waits for them, and re-layouts  9.44 us (2%)
    pallas_call x1, Pallas kernels, scatter_gradients(): pl.pallas_call(functools.partial(scatter_kernel, chunks, by_z), out_shape...  101 us
    pallas_call x1, Pallas kernels, attend_back_heads(): pl.pallas_call(functools.partial(attend_back_kernel, align), out_shape=ja...  97.7 us
    pallas_call x1, Pallas kernels, feed_forward(): pl.pallas_call(feed_forward_kernel, out_shape=(jax.ShapeDtypeStruct(token...  74.7 us
    pallas_call x1, Pallas kernels, gather_tokens(): pl.pallas_call(functools.partial(gather_kernel, chunks, by_z), out_shape=...  70.9 us
    pallas_call x2, Pallas kernels, exchange(): pl.pallas_call(exchange_kernel, out_shape=jax.ShapeDtypeStruct(blocks.sha...  69.9 us
    pallas_call x1, Pallas kernels, gather_rows(): pl.pallas_call(functools.partial(gather_rows_kernel, chunks, by_z), out_s...  44.2 us
    pallas_call x1, Pallas kernels, attend_heads(): pl.pallas_call(functools.partial(attend_kernel, window, align), out_shape...  40.4 us
    pallas_call x1, Pallas kernels, project_heads(): pl.pallas_call(project_kernel, out_shape=(head_shape, head_shape, head_sh...  15.1 us
  transfers between devices with their start and end apart: 5, of which 0 were waited for; matrix products, arithmetic and copies ran while one was open for 2% of the time, Pallas kernels for 72%

commit v1 on v0

--- a/solution.py
+++ b/solution.py
@@ -407,10 +407,10 @@
     def own(which, chunk, slot, device):
         return go(tok_ref.at[which, rows(chunk)], all_ref.at[me, rows(chunk)], slot * chunks + chunk, device)
 
-    crossing = [own(1 - half, chunk, 0, partner) for chunk in range(chunks)]
-    own_y, own_z = [], []
+    own_y, own_z, crossing = [], [], []
     for chunk in range(chunks):
         own_y.append(own(half, chunk, 1, y_near))
+        crossing.append(own(1 - half, chunk, 0, partner))
         own_z.append(own(half, chunk, 2, z_near))
     weights = []
     for step in range(1, shards):
@@ -482,7 +482,7 @@
         copy.wait_send()
 
 
-def gather_tokens(tokens, w_part, norms, place, freq, shards, chunks=8, by_z=3):
+def gather_tokens(tokens, w_part, norms, place, freq, shards, chunks=8, by_z=2):
     seqs, rows, width = tokens.shape
     anywhere = pl.BlockSpec(memory_space=pl.ANY)
     vmem = pl.BlockSpec(memory_space=pltpu.VMEM)
@@ -1420,10 +1420,10 @@
     def relay(device, chunk, slot, target):
         return go(band(device, chunk), band(device, chunk), slot * chunks + chunk, target)
 
-    crossing = [own(chunk, 0, partner) for chunk in range(chunks)]
-    own_y, own_z = [], []
+    own_y, own_z, crossing = [], [], []
     for chunk in range(chunks):
         own_y.append(own(chunk, 1, y_near))
+        crossing.append(own(chunk, 0, partner))
         own_z.append(own(chunk, 2, z_near))
     keep = pltpu.make_async_copy(own_ref, rows_ref.at[pl.ds(me * count, count)], kept)
     keep.start()
@@ -1452,7 +1452,7 @@
         copy.wait_send()
 
 
-def gather_rows(owned, chunks=8, by_z=3):
+def gather_rows(owned, chunks=8, by_z=2):
     hbm = pl.BlockSpec(memory_space=pltpu.HBM)
     dma = pltpu.SemaphoreType.DMA
     return pl.pallas_call(

time: 555 us -> 551 us (level)
  Pallas kernels: 521 us -> 513 us
where the time goes in v1:
time: 551 us; the launch traced here: 543 us
  Pallas kernels  513 us (93%)
  between operations  14.1 us (3%)
  local copies, waits for them, and re-layouts  9.44 us (2%)
    pallas_call x1, Pallas kernels, scatter_gradients(): pl.pallas_call(functools.partial(scatter_kernel, chunks, by_z), out_shape...  105 us
    pallas_call x1, Pallas kernels, attend_back_heads(): pl.pallas_call(functools.partial(attend_back_kernel, align), out_shape=ja...  92.6 us
    pallas_call x1, Pallas kernels, feed_forward(): pl.pallas_call(feed_forward_kernel, out_shape=(jax.ShapeDtypeStruct(token...  74.7 us
    pallas_call x2, Pallas kernels, exchange(): pl.pallas_call(exchange_kernel, out_shape=jax.ShapeDtypeStruct(blocks.sha...  71.5 us
    pallas_call x1, Pallas kernels, gather_tokens(): pl.pallas_call(functools.partial(gather_kernel, chunks, by_z), out_shape=...  66.7 us
    pallas_call x1, Pallas kernels, gather_rows(): pl.pallas_call(functools.partial(gather_rows_kernel, chunks, by_z), out_s...  43.3 us
    pallas_call x1, Pallas kernels, attend_heads(): pl.pallas_call(functools.partial(attend_kernel, window, align), out_shape...  36.9 us
    pallas_call x1, Pallas kernels, project_heads(): pl.pallas_call(project_kernel, out_shape=(head_shape, head_shape, head_sh...  15.4 us
  transfers between devices with their start and end apart: 5, of which 0 were waited for; matrix products, arithmetic and copies ran while one was open for 2% of the time, Pallas kernels for 72%

profile of v1, /device:TPU:20, one launch (start us, length us, event | category | flops | bytes accessed | tf_op | source)
XLA Modules:
  0.0 543.0 jit_solution(17798788305993068076)
XLA Ops:
  7.2 0.0 all-gather.5.cloned.1.call-start
  7.2 0.7 all-gather.5.cloned.1.call-update
  7.9 0.0 copy-start.4
  7.9 0.0 copy-start.2
  7.9 0.0 all-gather.11.cloned.1.call-start
  8.0 0.7 all-gather.11.cloned.1.call-update
  8.7 0.0 all-gather.7.cloned.1.call-start
  8.7 0.7 all-gather.7.cloned.1.call-update
  9.4 0.0 copy-start.5
  9.4 0.0 all-gather.9.cloned.1.call-start
  9.5 0.5 all-gather.9.cloned.1.call-update
  10.0 0.0 reduce-scatter.2.cloned.1.call-start
  10.1 0.0 copy-done.4
  10.1 0.6 fusion.2
  10.7 0.1 slice.45
  10.8 0.1 slice.46
  10.9 0.0 copy-done.2
  10.9 0.6 copy.30
  11.5 0.0 copy-start.6
  11.5 0.0 copy-start.7
  11.5 0.0 copy-start.8
  11.5 0.0 copy-start.9
  11.6 0.0 copy-done.5
  11.6 0.1 broadcast_multiply_fusion
  11.7 0.1 pad_maximum_fusion
  11.8 1.0 copy.33.w_ref
  12.8 0.0 copy-done.6
  12.8 0.0 copy-done.7
  12.8 0.0 copy-done.8
  12.8 0.0 copy-done.9
  12.9 0.6 broadcast_in_dim_tile.3.freq_ref
  13.4 0.6 maximum_convert_fusion.n_ref
  14.0 0.2 convert_reduce_fusion
  14.3 0.2 select_reduce_fusion
  14.5 0.6 subtract_convert_fusion.place_ref
  15.1 66.7 %gather_tokens.1 = (bf16[8,512,768]{2,1,0:T(8,128)(2,1)}, bf16[4,192,1152]{2,1,0:T(8,128)(2,1)}, f32[4,4,192]{2,1,0:T(4,128)}, f32[4096,128]{1,0:T(8,128)}) custom-call(bf16[2,512,768]{2,1,0:T(8,128)(2,1)} %tokens_ref.1, bf16[192,1152]{1,0:T(8,128)(2,1)} %copy.33.w_ref, f32[4,192]{1,0:T(4,128)} %maximum_convert_fusion.n_ref, ...), custom_call_target="tpu_custom_call" | custom-call | tf_op jit(solution)/shard_map/gather_tokens/pallas_call | solution.py:489
  81.9 0.2 convert_reduce_fusion.1
  82.1 0.5 subtract_minimum_fusion
  82.7 15.4 %project_heads.1 = (bf16[3,4096,128]{2,1,0:T(8,128)(2,1)}, bf16[3,4096,128]{2,1,0:T(8,128)(2,1)}, bf16[3,4096,128]{2,1,0:T(8,128)(2,1)}) custom-call(f32[8,1,512]{2,1,0:T(1,128)} %bitcast.26, f32[4096,128]{1,0:T(8,128)} %get-tuple-element.35.turn_ref, bf16[8,512,768]{2,1,0:T(8,128)(2,1)} %get-tuple-element.36.x_ref.x_hbm, bf16[768,1152]{1,0:T(8,128)(2,1)} %bitcast.18), custom_call_target="tpu_custom_call" | custom-call | flops 7247757312 | bytes 17825792 | tf_op jit(solution)/shard_map/project_heads/pallas_call | solution.py:547
  98.1 36.9 %attend_heads.1 = (f32[3,4096,128]{2,1,0:T(8,128)}, bf16[8,768,128]{2,1,0:T(8,128)(2,1)}) custom-call(s32[8]{0:T(128)} %get-tuple-element.82.low_ref, s32[8]{0:T(128)} %get-tuple-element.83.count_ref, bf16[3,4096,128]{2,1,0:T(8,128)(2,1)} %get-tuple-element.38.q_ref, bf16[3,4096,128]{2,1,0:T(8,128)(2,1)} %get-tuple-element.39.k_ref, ...), custom_call_target="tpu_custom_call" | custom-call | flops 12884901888 | bytes 15728640 | tf_op jit(solution)/shard_map/attend_heads/pallas_call | solution.py:610
  134.9 0.0 copy-start.3
  134.9 35.2 %exchange.2.joined_ref = bf16[8,768,128]{2,1,0:T(8,128)(2,1)} custom-call(bf16[8,768,128]{2,1,0:T(8,128)(2,1)} %get-tuple-element.41.sent_ref), custom_call_target="tpu_custom_call" | custom-call | tf_op jit(solution)/shard_map/exchange/pallas_call | solution.py:1551
  170.1 0.0 copy-done.3
  170.1 0.7 reshape.89.norms_ref
  170.8 0.0 all-gather.5.cloned.1.call-done.out_hbm
  170.8 0.0 all-gather.11.cloned.1.call-done.down_hbm
  170.8 0.0 all-gather.7.cloned.1.call-done.gate_hbm
  170.8 0.0 all-gather.9.cloned.1.call-done.up_hbm
  170.8 74.7 %feed_forward.1 = (bf16[2,512,768]{2,1,0:T(8,128)(2,1)}, bf16[8,768,128]{2,1,0:T(8,128)(2,1)}, f32[2,512,768]{2,1,0:T(8,128)}, f32[4,768]{1,0:T(4,128)}, bf16[4,2560,768]{2,1,0:T(8,128)(2,1)}) custom-call(bf16[2,512,768]{2,1,0:T(8,128)(2,1)} %tokens_ref.1, bf16[8,768,128]{2,1,0:T(8,128)(2,1)} %exchange.2.joined_ref, bf16[2,512,768]{2,1,0:T(8,128)(2,1)} %cot_ref.1, ...), custom_call_target="tpu_custom_call" | custom-call | flops 47110422528 | bytes 46399488 | tf_op jit(solution)/shard_map/feed_forward/pallas_call | solution.py:1350
  245.5 0.0 copy-start
  245.5 0.0 reduce-scatter.2.cloned.1.call-update
  245.6 1.4 copy-done
  247.0 0.3 fusion.3
  247.4 1.9 concatenate.7.w_ref
  249.3 36.3 %exchange.3.dout_ref = bf16[8,768,128]{2,1,0:T(8,128)(2,1)} custom-call(bf16[8,768,128]{2,1,0:T(8,128)(2,1)} %get-tuple-element.45.sent_ref), custom_call_target="tpu_custom_call" | custom-call | tf_op jit(solution)/shard_map/exchange/pallas_call | solution.py:1551
  285.6 92.6 %attend_back_heads.1.d_hbm = bf16[8,512,576]{2,1,0:T(8,128)(2,1)} custom-call(s32[8]{0:T(128)} %get-tuple-element.61.low_ref, s32[8]{0:T(128)} %get-tuple-element.62.count_ref, bf16[3,4096,128]{2,1,0:T(8,128)(2,1)} %get-tuple-element.38.q_ref, f32[3,4096,128]{2,1,0:T(8,128)} %get-tuple-element.44.sum_ref, bf16[8,768,128]{2,1,0:T(8,128)(2,1)} %exchange.3.dout_ref, ...), custom_call_target="tpu_custom_call" | custom-call | flops 32212254720 | bytes 31457280 | tf_op jit(solution)/shard_map/attend_back_heads/pallas_call | solution.py:744
  378.3 105.3 %scatter_gradients.1 = (bf16[2,512,768]{2,1,0:T(8,128)(2,1)}, bf16[4,192,576]{2,1,0:T(8,128)(2,1)}, f32[4,768]{1,0:T(4,128)}) custom-call(bf16[8,512,576]{2,1,0:T(8,128)(2,1)} %attend_back_heads.1.d_hbm, bf16[8,512,768]{2,1,0:T(8,128)(2,1)} %get-tuple-element.36.x_ref.x_hbm, bf16[768,576]{1,0:T(8,128)(2,1)} %concatenate.7.w_ref, ...), custom_call_target="tpu_custom_call" | custom-call | flops 60000002048 | bytes 67108864 | tf_op jit(solution)/shard_map/scatter_gradients/pallas_call | solution.py:1053
  483.5 1.5 fusion.4
  485.0 0.0 reduce-scatter.2.cloned.1.call-done.own_ref
  485.0 43.3 %gather_rows.1.gate_rows.up_rows.down_rows.out_rows = bf16[2560,768]{1,0:T(8,128)(2,1)} custom-call(bf16[320,768]{1,0:T(8,128)(2,1)} %reduce-scatter.2.cloned.1.call-done.own_ref), custom_call_target="tpu_custom_call" | custom-call | tf_op jit(solution)/shard_map/gather_rows/pallas_call | solution.py:1458
  528.4 0.0 copy-start.1
  528.4 6.9 %unpack_gradients.1 = (f32[192,3072]{1,0:T(8,128)}, f32[192,3072]{1,0:T(8,128)}, f32[768,768]{1,0:T(8,128)}, f32[192,768]{1,0:T(8,128)}, f32[192,2304]{1,0:T(8,128)}) custom-call(bf16[2560,768]{1,0:T(8,128)(2,1)} %gather_rows.1.gate_rows.up_rows.down_rows.out_rows, bf16[2560,768]{1,0:T(8,128)(2,1)} %gather_rows.1.gate_rows.up_rows.down_rows.out_rows, ...), custom_call_target="tpu_custom_call" | custom-call | tf_op jit(solution)/shard_map/unpack_gradients/pallas_call | solution.py:1492
  535.3 0.0 copy-done.1
  535.3 1.1 copy.35
  (8 shorter events, 0.1 us)
Async XLA Ops:
  7.2 163.6 %all-gather.5.cloned.1.call-start = ((), (), s32[]{:S(2)}) async-start(), calls=%async_computation.1 | async-start | bytes 1474560 | tf_op jit(solution)/shard_map/all_gather | solution.py:1593
  7.9 2.2 copy-start.4
  7.9 3.0 copy-start.2
  7.9 162.9 %all-gather.11.cloned.1.call-start = ((), (), s32[]{:S(2)}) async-start(), calls=%async_computation.4 | async-start | bytes 5898240 | tf_op jit(solution)/shard_map/all_gather | solution.py:1593
  8.7 162.1 %all-gather.7.cloned.1.call-start = ((), (), s32[]{:S(2)}) async-start(), calls=%async_computation.2 | async-start | bytes 5898240 | tf_op jit(solution)/shard_map/all_gather | solution.py:1593
  9.4 2.1 copy-start.5
  9.4 161.4 %all-gather.9.cloned.1.call-start = ((), (), s32[]{:S(2)}) async-start(), calls=%async_computation.3 | async-start | bytes 5898240 | tf_op jit(solution)/shard_map/all_gather | solution.py:1593
  10.0 475.0 %reduce-scatter.2.cloned.1.call-start = ((), (), s32[]{:S(2)}) async-start(), calls=%async_computation.5 | async-start | bytes 16220160 | tf_op jit(solution)/shard_map/reduce_scatter | solution.py:1614
  11.5 1.3 copy-start.6
  11.5 1.3 copy-start.7
  11.5 1.3 copy-start.8
  11.5 1.3 copy-start.9
  134.9 35.2 %copy-start.3 = (f32[4,4,192]{2,1,0:T(4,128)S(1)}, f32[4,4,192]{2,1,0:T(4,128)}, u32[]{:S(2)}) copy-start(f32[4,4,192]{2,1,0:T(4,128)} %get-tuple-element.42) | copy-start | bytes 36868
  245.5 1.5 copy-start
  528.4 6.9 %copy-start.1 = (bf16[2,512,768]{2,1,0:T(8,128)(2,1)S(1)}, bf16[2,512,768]{2,1,0:T(8,128)(2,1)}, u32[]{:S(2)}) copy-start(bf16[2,512,768]{2,1,0:T(8,128)(2,1)} %get-tuple-element.98) | copy-start | bytes 4718596
Sparse Core Ops, SparseCore 0:
  9.5 24.8 all-gather.4
  36.0 37.4 all-gather.10
  75.0 37.4 all-gather.6
  113.9 37.5 all-gather.8
  245.7 214.4 reduce-scatter.1
